TPU v7x, 128 devices: a whole 4x4x4 slice. The times are simulated.
128 devices in a mesh: row: 8 (over z_lo, y), col: 16 (over z_hi, x, core).
Axes of the slice: x: 4, y: 4, z: 4 (z_hi: 2, z_lo: 2; z = z_hi * 2 + z_lo), core: 2. Of those that a mesh axis runs over, the one named last changes fastest.
Arguments:
- initial_field: float32 [256, 256, 256], P(('row', 'col')), may hold values from -5 to 5
Outputs:
- advanced_field: float32 [256, 256, 256], P(('row', 'col'))
All inputs are finite; a program needn't handle non-finite values.
Results may differ from a plain program's by a relative error of at most 0.0003.
Values sent between devices are 32-bit elements; how exact they have to be, the bound alone decides.
No kernel may reach another device: no remote copies, remote signals or barrier semaphores. Data moves between devices by JAX's collectives and lax.ppermute only.
A program may use at most 64 MiB of HBM per device.

v0:
```python
import functools
import math

import jax
import jax.numpy as jnp
import numpy as np
from jax import lax
from jax.experimental import pallas as pl
from jax.experimental.pallas import tpu as pltpu
from jax.sharding import PartitionSpec as P

growth_rate = 0.3
quadratic = 1.0
time_step = 0.2
wave_scale = 4.0

N = 256
H = 128
BOTH = ("row", "col")
F32 = jnp.float32
BF16 = jnp.bfloat16


def tables():
    n = np.arange(N)
    j = np.arange(H)
    angle = 2.0 * np.pi / N * ((j[:, None] * n[None, :]) % N)
    cosine = np.cos(angle)
    sine = np.sin(angle)
    alternate = 1.0 - 2.0 * (n % 2)
    sine_alt = sine.copy()
    sine_alt[0] = alternate
    forward_y = np.concatenate([cosine, sine_alt])
    inverse_y = forward_y.T / N
    order = np.concatenate([np.arange(0, N, 2), np.arange(1, N, 2)])
    forward_x = forward_y[:, order]
    inverse_x = inverse_y[order]
    minus = -sine
    minus[0] = alternate
    forward_z = np.concatenate([cosine, minus]).T
    weight = np.where(j == 0, 1.0, 2.0)[:, None] / N
    inverse_z = np.concatenate([cosine * weight, minus * weight])
    return dict(fx=forward_x, ix=inverse_x, fy=forward_y, iy=inverse_y, fz=forward_z, iz=inverse_z)


def split_table(table):
    high = np.asarray(table, np.float32).astype(jnp.bfloat16)
    low = (table - high.astype(np.float64)).astype(np.float32).astype(jnp.bfloat16)
    return np.stack([high, low])


def split(values):
    high = values.astype(BF16)
    low = (values - high.astype(F32)).astype(BF16)
    return high, low


def dot(left, right):
    return jnp.dot(left, right, preferred_element_type=F32)


def table_left(table, values):
    high, low = split(values)
    return dot(table[0], high) + (dot(table[0], low) + dot(table[1], high))


def table_right(values, table):
    high, low = split(values)
    return dot(high, table[0]) + (dot(low, table[0]) + dot(high, table[1]))


def grid_of(axis):
    return lax.broadcasted_iota(jnp.int32, (H, H), axis)


def quarters(whole):
    return whole[:H, :H], whole[:H, H:], whole[H:, :H], whole[H:, H:]


def joined(top_left, top_right, bottom_left, bottom_right):
    return jnp.concatenate(
        [
            jnp.concatenate([top_left, top_right], axis=1),
            jnp.concatenate([bottom_left, bottom_right], axis=1),
        ],
        axis=0,
    )


def tile_rows(ref, slot):
    return ref[pl.ds(slot, H, stride=ref.shape[0] // H), :]


def put_rows(ref, slot, values):
    ref[pl.ds(slot, H, stride=ref.shape[0] // H), :] = values


def reaction(values):
    return quadratic * values * values - values * values * values


def send_modes(whole, send, base):
    cre, cim, sre, sim = quarters(whole)
    lane0 = grid_of(1) == 0
    row0 = grid_of(0) == 0
    corner = lane0 & row0
    o0re = jnp.where(lane0 | row0, cre, cre + sim)
    o0im = jnp.where(lane0, -sre, cim - sre)
    o0im = jnp.where(row0, cim, o0im)
    o0im = jnp.where(corner, sim, o0im)
    o1re = jnp.where(row0, sre, cre - sim)
    o1re = jnp.where(lane0, cim, o1re)
    o1im = jnp.where(lane0, -sim, cim + sre)
    o1im = jnp.where(row0, sim, o1im)
    o1im = jnp.where(corner, sre, o1im)
    put_rows(send, base + 0, o0re)
    put_rows(send, base + 1, o0im)
    put_rows(send, base + 2, o1re)
    put_rows(send, base + 3, o1im)


def got_modes(got, base):
    s0re = tile_rows(got, base + 0)
    s0im = tile_rows(got, base + 1)
    s1re = tile_rows(got, base + 2)
    s1im = tile_rows(got, base + 3)
    lane0 = grid_of(1) == 0
    row0 = grid_of(0) == 0
    corner = lane0 & row0
    pre = jnp.where(lane0, 2.0 * s0re, s0re + s1re)
    pre = jnp.where(row0, s0re, pre)
    pim = jnp.where(lane0, 2.0 * s1re, s0im + s1im)
    pim = jnp.where(row0, s0im, pim)
    pim = jnp.where(corner, s1re, pim)
    mre = jnp.where(lane0, -2.0 * s0im, s1im - s0im)
    mre = jnp.where(row0, s1re, mre)
    mre = jnp.where(corner, s1im, mre)
    mim = jnp.where(lane0, -2.0 * s1im, s0re - s1re)
    mim = jnp.where(row0, s1im, mim)
    mim = jnp.where(corner, s0im, mim)
    return joined(pre, pim, mre, mim)


def from_messages(got, base, iy, iz):
    modes = got_modes(got, base)
    half = table_left(iy, modes)
    return table_right(half, iz)


def to_messages(values, send, base, fz, fy):
    half = table_right(values, fz)
    send_modes(table_left(fy, half), send, base)


def first_kernel(field, fz, fy, send):
    for row in range(2):
        values = field[row]
        to_messages(values, send, 4 * row, fz, fy)
        to_messages(reaction(values), send, 8 + 4 * row, fz, fy)


def middle_kernel(got, iy, iz, fz, fy, send):
    for row in range(2):
        values = from_messages(got, 4 * row, iy, iz)
        to_messages(reaction(values), send, 4 * row, fz, fy)


def last_kernel(got, iy, iz, field):
    for row in range(2):
        field[row] = from_messages(got, 4 * row, iy, iz)


def special_lane(slot):
    if slot:
        return None
    device = lax.axis_index(BOTH)
    lane = grid_of(1) + jnp.where(device == 0, 0, H)
    return (lane == 0) & (grid_of(0) != 0)


def spectrum_of(got, slot, fx, field=0):
    at = 8 * field + 2 * slot
    column = joined(*(tile_rows(got, at + k) for k in (0, 1, 4, 5)))
    cre, cim, sre, sim = quarters(table_left(fx, column))
    row0 = grid_of(0) == 0
    tre = jnp.where(row0, cre, cre + sim)
    tim = jnp.where(row0, cim, cim - sre)
    bre = jnp.where(row0, sre, cre - sim)
    bim = jnp.where(row0, sim, cim + sre)
    special = special_lane(slot)
    if special is not None:
        tre = jnp.where(special, cre, tre)
        tim = jnp.where(special, -sre, tim)
        bre = jnp.where(special, cim, bre)
        bim = jnp.where(special, -sim, bim)
    return tre, tim, bre, bim


def spectrum_to(parts, slot, ix, send):
    tre, tim, bre, bim = parts
    row0 = grid_of(0) == 0
    pre = jnp.where(row0, tre, tre + bre)
    pim = jnp.where(row0, tim, tim + bim)
    mre = jnp.where(row0, bre, bim - tim)
    mim = jnp.where(row0, bim, tre - bre)
    special = special_lane(slot)
    if special is not None:
        pre = jnp.where(special, 2.0 * tre, pre)
        pim = jnp.where(special, 2.0 * bre, pim)
        mre = jnp.where(special, -2.0 * tim, mre)
        mim = jnp.where(special, -2.0 * bim, mim)
    out = table_left(ix, joined(pre, pim, mre, mim))
    a, b, c, d = quarters(out)
    put_rows(send, 2 * slot, a)
    put_rows(send, 2 * slot + 1, b)
    put_rows(send, 2 * slot + 4, c)
    put_rows(send, 2 * slot + 5, d)


def plane_of(slot, half, part):
    if slot:
        return 2 + half
    return (4 if part else 0) + half


def each_part():
    for half in range(2):
        for part in range(2):
            yield 2 * half + part, half, part


def spectral_first(got, factors, fx, ix, send, keep, base, total):
    for slot in range(2):
        state = spectrum_of(got, slot, fx)
        react = spectrum_of(got, slot, fx, field=1)
        nexts = []
        for k, half, part in each_part():
            plane = plane_of(slot, half, part)
            e_half = factors[0, plane]
            q_half = factors[1, plane]
            kept = e_half * state[k]
            turn = q_half * react[k]
            first = kept + turn
            keep[4 * slot + k] = kept
            base[4 * slot + k] = e_half * first - turn
            total[4 * slot + k] = factors[2, plane] * state[k] + factors[3, plane] * react[k]
            nexts.append(first)
        spectrum_to(nexts, slot, ix, send)


def spectral_middle(got, factors, kept, total, fx, ix, send, total_out, *, twice):
    for slot in range(2):
        react = spectrum_of(got, slot, fx)
        nexts = []
        for k, half, part in each_part():
            plane = plane_of(slot, half, part)
            turn = factors[1, plane] * react[k]
            if twice:
                turn = 2.0 * turn
            nexts.append(kept[4 * slot + k] + turn)
            total_out[4 * slot + k] = total[4 * slot + k] + 2.0 * factors[4, plane] * react[k]
        spectrum_to(nexts, slot, ix, send)


def spectral_last(got, factors, total, fx, ix, send):
    for slot in range(2):
        react = spectrum_of(got, slot, fx)
        nexts = []
        for k, half, part in each_part():
            plane = plane_of(slot, half, part)
            nexts.append(total[4 * slot + k] + factors[5, plane] * react[k])
        spectrum_to(nexts, slot, ix, send)


def phi_values(argument, degrees):
    within = jnp.abs(argument) < 1.0
    inside = jnp.where(within, argument, 0.0)
    outside = jnp.where(within, 2.0, argument)
    series = []
    for degree in degrees:
        running = jnp.zeros_like(argument) + 1.0 / math.factorial(11 + degree)
        for exponent in range(10, -1, -1):
            running = running * inside + 1.0 / math.factorial(exponent + degree)
        series.append(running)
    growth = jnp.exp(outside)
    closed = [(growth - 1.0) / outside]
    if len(degrees) > 1:
        square = outside * outside
        closed.append((growth - 1.0 - outside) / square)
        closed.append((growth - 1.0 - outside - 0.5 * square) / (square * outside))
    return [jnp.where(within, s, c) for s, c in zip(series, closed)]


def factor_kernel(factors):
    device = lax.axis_index(BOTH)
    square = H * H
    row = grid_of(0)
    lane = grid_of(1)
    own = device * device
    alone = jnp.where(device == 0, 1, 0)
    for plane in range(6):
        half = plane % 2
        slot = 1 if plane // 2 == 1 else 0
        imaginary = plane // 2 == 2
        modes = row * row
        if half:
            modes = jnp.where(row == 0, square, modes)
        lane0 = lane == 0
        if slot:
            modes = modes + own + alone * square
            modes = modes + jnp.where(lane0, (1 - alone) * square, lane * lane)
        else:
            modes = modes + own + lane * lane
            pair = lane0 & (row == 0) if not half else (lane0 & (row != 0))
            if imaginary and half:
                pair = lane0
            if half or imaginary:
                modes = modes + jnp.where(pair, alone * (2 * square), 0)
        ksq = modes.astype(F32) * (wave_scale / N) ** 2
        lin = growth_rate - (1.0 - ksq) * (1.0 - ksq)
        scaled = time_step * lin
        (half_phi,) = phi_values(0.5 * scaled, (1,))
        first, second, third = phi_values(scaled, (1, 2, 3))
        factors[0, plane] = jnp.exp(0.5 * scaled)
        factors[1, plane] = 0.5 * time_step * half_phi
        factors[2, plane] = jnp.exp(scaled)
        factors[3, plane] = time_step * (first - 3.0 * second + 4.0 * third)
        factors[4, plane] = time_step * (second - 2.0 * third)
        factors[5, plane] = time_step * (4.0 * third - second)


def shape(*dims):
    return jax.ShapeDtypeStruct(dims, F32)


def call(kernel, outs, *args, name):
    vmem = pl.BlockSpec(memory_space=pltpu.VMEM)
    single = not isinstance(outs, tuple)
    return pl.pallas_call(
        kernel,
        out_shape=outs,
        in_specs=[vmem] * len(args),
        out_specs=vmem if single else tuple(vmem for _ in outs),
        name=name,
    )(*args)


def move(send):
    tiles = send.reshape(H, send.shape[0] // H, H)
    out = lax.all_to_all(tiles, BOTH, split_axis=0, concat_axis=0, tiled=True)
    return out.reshape(send.shape)


def body(tabs, field):
    fx, ix, fy, iy, fz, iz = (tabs[k] for k in ("fx", "ix", "fy", "iy", "fz", "iz"))
    message = shape(8 * H, H)
    spectrum = shape(8, H, H)
    factors = call(factor_kernel, shape(6, 6, H, H), name="factors")
    send = call(first_kernel, shape(16 * H, H), field, fz, fy, name="first")
    got = move(send)
    send, keep, base, total = call(
        spectral_first, (message, spectrum, spectrum, spectrum), got, factors, fx, ix, name="spectral_first"
    )

    def physical(send):
        return move(call(middle_kernel, message, move(send), iy, iz, fz, fy, name="physical"))

    for kept, twice in ((keep, False), (base, True)):
        got = physical(send)
        send, total = call(
            functools.partial(spectral_middle, twice=twice),
            (message, spectrum),
            got, factors, kept, total, fx, ix,
            name="spectral_middle",
        )
    got = physical(send)
    send = call(spectral_last, message, got, factors, total, fx, ix, name="spectral_last")
    return call(last_kernel, shape(2, N, N), move(send), iy, iz, name="last")


def solution(mesh):
    tabs = {k: split_table(v) for k, v in tables().items()}
    placed = P(BOTH, None, None)

    def run(initial_field):
        return body({k: jnp.asarray(v) for k, v in tabs.items()}, initial_field)

    return jax.shard_map(run, mesh=mesh, in_specs=(placed,), out_specs=placed, check_vma=False)
```

profile of v0, /device:TPU:1, one launch (start us, length us, event | category | flops | bytes accessed | tf_op | source)
XLA Modules:
  0.0 200.2 jit_solution(16005062958640635447)
XLA Ops:
  0.0 3.6 %first.1 = f32[2048,128]{1,0:T(8,128)} custom-call(f32[2,256,256]{2,1,0:T(8,128)} %field.1, bf16[2,256,256]{2,1,0:T(8,128)(2,1)} %constant.16.clone.fz, bf16[2,256,256]{2,1,0:T(8,128)(2,1)} %constant.14.clone.fy), custom_call_target="tpu_custom_call" | custom-call | tf_op jit(solution)/shard_map/first/pallas_call | solution.py:339
  3.6 11.5 %all-to-all-start = ((f32[128,16,128]{2,1,0:T(8,128)}), f32[128,16,128]{2,1,0:T(8,128)S(1)}, u32[]{:S(2)}, u32[]{:S(2)}) async-start(f32[128,16,128]{2,1,0:T(8,128)} %bitcast.16), calls=%async_computation | async-start | bytes 2097152 | tf_op jit(solution)/shard_map/all_to_all | solution.py:350
  15.1 2.4 %factors.1 = f32[6,6,128,128]{3,2,1,0:T(8,128)} custom-call(), custom_call_target="tpu_custom_call" | custom-call | tf_op jit(solution)/shard_map/factors/pallas_call | solution.py:339
  17.6 16.5 %all-to-all-done = f32[128,16,128]{2,1,0:T(8,128)S(1)} async-done(((f32[128,16,128]{2,1,0:T(8,128)}), f32[128,16,128]{2,1,0:T(8,128)S(1)}, u32[]{:S(2)}, u32[]{:S(2)}) %all-to-all-start) | async-done | bytes 1048608 | tf_op jit(solution)/shard_map/all_to_all | solution.py:350
  34.1 0.0 copy-start
  34.1 1.0 copy-done
  35.0 4.5 %spectral_first.1 = (f32[1024,128]{1,0:T(8,128)}, f32[8,128,128]{2,1,0:T(8,128)}, f32[8,128,128]{2,1,0:T(8,128)}, f32[8,128,128]{2,1,0:T(8,128)}) custom-call(f32[2048,128]{1,0:T(8,128)} %bitcast.17, f32[6,6,128,128]{3,2,1,0:T(8,128)} %factors.1, bf16[2,256,256]{2,1,0:T(8,128)(2,1)} %constant.12.clone.fx, bf16[2,256,256]{2,1,0:T(8,128)(2,1)} %constant.13.clone.ix), custom_call_target="tpu_custom_call" | custom-call | tf_op jit(solution)/shard_map/spectral_first/pallas_call | solution.py:339
  39.6 19.2 %all_to_all.40 = f32[128,8,128]{2,1,0:T(8,128)} all-to-all(f32[128,8,128]{2,1,0:T(8,128)} %bitcast.29), channel_id=1, replica_groups=mesh['row'=8,'col'=16] {'row','col'}, dimensions={0} | all-to-all | bytes 1048576 | tf_op jit(solution)/shard_map/all_to_all | solution.py:350
  58.8 4.2 %physical.3 = f32[1024,128]{1,0:T(8,128)} custom-call(f32[1024,128]{1,0:T(8,128)} %bitcast.25, bf16[2,256,256]{2,1,0:T(8,128)(2,1)} %constant.15.clone.iy, bf16[2,256,256]{2,1,0:T(8,128)(2,1)} %constant.17.clone.iz, bf16[2,256,256]{2,1,0:T(8,128)(2,1)} %constant.16.clone.fz, bf16[2,256,256]{2,1,0:T(8,128)(2,1)} %constant.14.clone.fy), custom_call_target="tpu_custom_call" | custom-call | tf_op jit(solution)/shard_map/physical/pallas_call | solution.py:339
  63.0 19.0 %all_to_all.41 = f32[128,8,128]{2,1,0:T(8,128)} all-to-all(f32[128,8,128]{2,1,0:T(8,128)} %bitcast.26), channel_id=1, replica_groups=mesh['row'=8,'col'=16] {'row','col'}, dimensions={0} | all-to-all | bytes 1048576 | tf_op jit(solution)/shard_map/all_to_all | solution.py:350
  82.0 4.0 %spectral_middle.2 = (f32[1024,128]{1,0:T(8,128)}, f32[8,128,128]{2,1,0:T(8,128)}) custom-call(f32[1024,128]{1,0:T(8,128)} %bitcast.20, f32[6,6,128,128]{3,2,1,0:T(8,128)} %factors.1, f32[8,128,128]{2,1,0:T(8,128)} %get-tuple-element.14.kept, f32[8,128,128]{2,1,0:T(8,128)} %get-tuple-element.15.total, bf16[2,256,256]{2,1,0:T(8,128)(2,1)} %constant.12.clone.fx, ...), custom_call_target="tpu_custom_call" | custom-call | tf_op jit(solution)/shard_map/spectral_middle/pallas_call | solution.py:339
  86.0 19.0 %all_to_all.42 = f32[128,8,128]{2,1,0:T(8,128)} all-to-all(f32[128,8,128]{2,1,0:T(8,128)} %bitcast.30), channel_id=1, replica_groups=mesh['row'=8,'col'=16] {'row','col'}, dimensions={0} | all-to-all | bytes 1048576 | tf_op jit(solution)/shard_map/all_to_all | solution.py:350
  105.0 4.2 %physical.4 = f32[1024,128]{1,0:T(8,128)} custom-call(f32[1024,128]{1,0:T(8,128)} %bitcast.27, bf16[2,256,256]{2,1,0:T(8,128)(2,1)} %constant.15.clone.iy, bf16[2,256,256]{2,1,0:T(8,128)(2,1)} %constant.17.clone.iz, bf16[2,256,256]{2,1,0:T(8,128)(2,1)} %constant.16.clone.fz, bf16[2,256,256]{2,1,0:T(8,128)(2,1)} %constant.14.clone.fy), custom_call_target="tpu_custom_call" | custom-call | tf_op jit(solution)/shard_map/physical/pallas_call | solution.py:339
  109.2 19.1 %all_to_all.43 = f32[128,8,128]{2,1,0:T(8,128)} all-to-all(f32[128,8,128]{2,1,0:T(8,128)} %bitcast.28), channel_id=1, replica_groups=mesh['row'=8,'col'=16] {'row','col'}, dimensions={0} | all-to-all | bytes 1048576 | tf_op jit(solution)/shard_map/all_to_all | solution.py:350
  128.3 4.0 %spectral_middle.3 = (f32[1024,128]{1,0:T(8,128)}, f32[8,128,128]{2,1,0:T(8,128)}) custom-call(f32[1024,128]{1,0:T(8,128)} %bitcast.18, f32[6,6,128,128]{3,2,1,0:T(8,128)} %factors.1, f32[8,128,128]{2,1,0:T(8,128)} %get-tuple-element.17.kept, f32[8,128,128]{2,1,0:T(8,128)} %get-tuple-element.18.total, bf16[2,256,256]{2,1,0:T(8,128)(2,1)} %constant.12.clone.fx, ...), custom_call_target="tpu_custom_call" | custom-call | tf_op jit(solution)/shard_map/spectral_middle/pallas_call | solution.py:339
  132.2 19.0 %all_to_all.44 = f32[128,8,128]{2,1,0:T(8,128)} all-to-all(f32[128,8,128]{2,1,0:T(8,128)} %bitcast.31), channel_id=1, replica_groups=mesh['row'=8,'col'=16] {'row','col'}, dimensions={0} | all-to-all | bytes 1048576 | tf_op jit(solution)/shard_map/all_to_all | solution.py:350
  151.3 4.2 %physical.5 = f32[1024,128]{1,0:T(8,128)} custom-call(f32[1024,128]{1,0:T(8,128)} %bitcast.23, bf16[2,256,256]{2,1,0:T(8,128)(2,1)} %constant.15.clone.iy, bf16[2,256,256]{2,1,0:T(8,128)(2,1)} %constant.17.clone.iz, bf16[2,256,256]{2,1,0:T(8,128)(2,1)} %constant.16.clone.fz, bf16[2,256,256]{2,1,0:T(8,128)(2,1)} %constant.14.clone.fy), custom_call_target="tpu_custom_call" | custom-call | tf_op jit(solution)/shard_map/physical/pallas_call | solution.py:339
  155.5 19.0 %all_to_all.45 = f32[128,8,128]{2,1,0:T(8,128)} all-to-all(f32[128,8,128]{2,1,0:T(8,128)} %bitcast.24), channel_id=1, replica_groups=mesh['row'=8,'col'=16] {'row','col'}, dimensions={0} | all-to-all | bytes 1048576 | tf_op jit(solution)/shard_map/all_to_all | solution.py:350
  174.5 3.8 %spectral_last.1 = f32[1024,128]{1,0:T(8,128)} custom-call(f32[1024,128]{1,0:T(8,128)} %bitcast.19, f32[6,6,128,128]{3,2,1,0:T(8,128)} %factors.1, f32[8,128,128]{2,1,0:T(8,128)} %get-tuple-element.20.total, bf16[2,256,256]{2,1,0:T(8,128)(2,1)} %constant.12.clone.fx, bf16[2,256,256]{2,1,0:T(8,128)(2,1)} %constant.13.clone.ix), custom_call_target="tpu_custom_call" | custom-call | tf_op jit(solution)/shard_map/spectral_last/pallas_call | solution.py:339
  178.3 19.1 %all_to_all.46 = f32[128,8,128]{2,1,0:T(8,128)} all-to-all(f32[128,8,128]{2,1,0:T(8,128)} %bitcast.21), channel_id=1, replica_groups=mesh['row'=8,'col'=16] {'row','col'}, dimensions={0} | all-to-all | bytes 1048576 | tf_op jit(solution)/shard_map/all_to_all | solution.py:350
  197.4 2.8 %last.1 = f32[2,256,256]{2,1,0:T(8,128)} custom-call(f32[1024,128]{1,0:T(8,128)} %bitcast.22, bf16[2,256,256]{2,1,0:T(8,128)(2,1)} %constant.15.clone.iy, bf16[2,256,256]{2,1,0:T(8,128)(2,1)} %constant.17.clone.iz), custom_call_target="tpu_custom_call" | custom-call | tf_op jit(solution)/shard_map/last/pallas_call | solution.py:339
Async XLA Ops:
  3.6 30.4 %all-to-all-start = ((f32[128,16,128]{2,1,0:T(8,128)}), f32[128,16,128]{2,1,0:T(8,128)S(1)}, u32[]{:S(2)}, u32[]{:S(2)}) async-start(f32[128,16,128]{2,1,0:T(8,128)} %bitcast.16), calls=%async_computation | async-start | bytes 2097152 | tf_op jit(solution)/shard_map/all_to_all | solution.py:350
  34.1 1.0 copy-start
where the time goes:
time: 201 us; the launch traced here: 200 us
  blocking collectives  134 us (67%)
  Pallas kernels  37.7 us (19%)
  waiting for transfers between devices  16.5 us (8%)
  starting transfers between devices  11.5 us (6%)
    all_to_all x7, blocking collectives, move(): out = lax.all_to_all(tiles, BOTH, split_axis=0, concat_axis=0, tiled=True)  134 us
    pallas_call x10, Pallas kernels, call(): pl.pallas_call(kernel, out_shape=outs, in_specs=[vmem] * len(args), out_s...  37.7 us
    all_to_all x1, waiting for transfers between devices, move(): out = lax.all_to_all(tiles, BOTH, split_axis=0, concat_axis=0, tiled=True)  16.5 us
    all_to_all x1, starting transfers between devices, move(): out = lax.all_to_all(tiles, BOTH, split_axis=0, concat_axis=0, tiled=True)  11.5 us
  transfers between devices with their start and end apart: 1, of which 1 were waited for; matrix products, arithmetic and copies ran while one was open for 0% of the time, Pallas kernels for 1%

commit v1 on v0

--- a/solution.py
+++ b/solution.py
@@ -341,6 +341,7 @@
         out_shape=outs,
         in_specs=[vmem] * len(args),
         out_specs=vmem if single else tuple(vmem for _ in outs),
+        compiler_params=pltpu.CompilerParams(vmem_limit_bytes=16 << 20),
         name=name,
     )(*args)
 

time: 201 us -> 174 us (0.87)
  Pallas kernels: 37.7 us -> 15.8 us
  blocking collectives: 134 us -> 124 us
  local copies, waits for them, and re-layouts: 0.98 us -> 4.87 us
    pallas_call x10, Pallas kernels: 37.7 us -> 15.8 us  [call(): pl.pallas_call(kernel, out_shape=outs, in_specs=[vmem] * len(args), out_s...]
    all_to_all x7, blocking collectives: 134 us -> 124 us  [move(): out = lax.all_to_all(tiles, BOTH, split_axis=0, concat_axis=0, tiled=True)]
    unnamed x2 -> x22, local copies, waits for them, and re-layouts: 0.98 us -> 4.87 us
where the time goes in v1:
time: 174 us
  blocking collectives  124 us (71%)
  waiting for transfers between devices  17.9 us (10%)
  Pallas kernels  15.8 us (9%)
  starting transfers between devices  11.5 us (7%)
  local copies, waits for them, and re-layouts  4.87 us (3%)
    all_to_all x7, blocking collectives, move(): out = lax.all_to_all(tiles, BOTH, split_axis=0, concat_axis=0, tiled=True)  124 us
    all_to_all x1, waiting for transfers between devices, move(): out = lax.all_to_all(tiles, BOTH, split_axis=0, concat_axis=0, tiled=True)  17.9 us
    pallas_call x10, Pallas kernels, call(): pl.pallas_call(kernel, out_shape=outs, in_specs=[vmem] * len(args), out_s...  15.8 us
    all_to_all x1, starting transfers between devices, move(): out = lax.all_to_all(tiles, BOTH, split_axis=0, concat_axis=0, tiled=True)  11.5 us
    unnamed x22, local copies, waits for them, and re-layouts  4.87 us
  transfers between devices with their start and end apart: 1, of which 1 were waited for; matrix products, arithmetic and copies ran while one was open for 0% of the time, Pallas kernels for 1%

profile of v1, /device:TPU:1, one launch (start us, length us, event | category | flops | bytes accessed | tf_op | source)
XLA Modules:
  0.0 173.8 jit_solution(13333496201509701646)
XLA Ops:
  0.0 0.0 copy-start.6
  0.0 0.9 copy-done.6
  1.0 0.0 copy-start.8
  1.0 0.9 copy-done.8
  1.9 0.0 copy-start.10
  1.9 1.0 copy-done.10
  2.9 2.5 %first.1 = f32[2048,128]{1,0:T(8,128)} custom-call(f32[2,256,256]{2,1,0:T(8,128)S(1)} %copy-done.10, bf16[2,256,256]{2,1,0:T(8,128)(2,1)S(1)} %copy-done.6, bf16[2,256,256]{2,1,0:T(8,128)(2,1)S(1)} %copy-done.8), custom_call_target="tpu_custom_call" | custom-call | tf_op jit(solution)/shard_map/first/pallas_call | solution.py:339
  5.4 11.5 %all-to-all-start = ((f32[128,16,128]{2,1,0:T(8,128)}), f32[128,16,128]{2,1,0:T(8,128)S(1)}, u32[]{:S(2)}, u32[]{:S(2)}) async-start(f32[128,16,128]{2,1,0:T(8,128)} %bitcast), calls=%async_computation | async-start | bytes 2097152 | tf_op jit(solution)/shard_map/all_to_all | solution.py:351
  16.9 1.0 factors.1
  17.9 17.9 %all-to-all-done = f32[128,16,128]{2,1,0:T(8,128)S(1)} async-done(((f32[128,16,128]{2,1,0:T(8,128)}), f32[128,16,128]{2,1,0:T(8,128)S(1)}, u32[]{:S(2)}, u32[]{:S(2)}) %all-to-all-start) | async-done | bytes 1048608 | tf_op jit(solution)/shard_map/all_to_all | solution.py:351
  35.8 0.0 copy-start
  35.8 0.9 copy-done
  36.8 0.0 copy-start.2
  36.8 0.9 copy-done.2
  37.7 0.0 copy-start.4
  37.7 0.0 copy-start.5
  37.7 0.0 copy-start.7
  37.7 0.0 copy-start.9
  37.7 1.7 spectral_first.1
  39.4 0.0 copy-start.1
  39.4 0.0 copy-start.3
  39.4 17.8 %all_to_all.40 = f32[128,8,128]{2,1,0:T(8,128)S(1)} all-to-all(f32[128,8,128]{2,1,0:T(8,128)S(1)} %bitcast.28), channel_id=1, replica_groups=mesh['row'=8,'col'=16] {'row','col'}, dimensions={0} | all-to-all | bytes 1048576 | tf_op jit(solution)/shard_map/all_to_all | solution.py:351
  57.2 0.0 copy-done.4
  57.2 0.0 copy-done.5
  57.2 0.0 copy-done.7
  57.2 0.0 copy-done.9
  57.2 2.0 %physical.3 = f32[1024,128]{1,0:T(8,128)S(1)} custom-call(f32[1024,128]{1,0:T(8,128)S(1)} %bitcast.24, bf16[2,256,256]{2,1,0:T(8,128)(2,1)S(1)} %copy-done.5, bf16[2,256,256]{2,1,0:T(8,128)(2,1)S(1)} %copy-done.4, bf16[2,256,256]{2,1,0:T(8,128)(2,1)S(1)} %copy-done.7, bf16[2,256,256]{2,1,0:T(8,128)(2,1)S(1)} %copy-done.9), custom_call_target="tpu_custom_call" | custom-call | tf_op jit(solution)/shard_map/physical/pallas_call | solution.py:339
  59.3 17.6 %all_to_all.41 = f32[128,8,128]{2,1,0:T(8,128)S(1)} all-to-all(f32[128,8,128]{2,1,0:T(8,128)S(1)} %bitcast.25), channel_id=1, replica_groups=mesh['row'=8,'col'=16] {'row','col'}, dimensions={0} | all-to-all | bytes 1048576 | tf_op jit(solution)/shard_map/all_to_all | solution.py:351
  76.9 0.0 copy-done.1
  76.9 0.0 copy-done.3
  76.9 1.0 spectral_middle.2
  77.9 17.6 %all_to_all.42 = f32[128,8,128]{2,1,0:T(8,128)S(1)} all-to-all(f32[128,8,128]{2,1,0:T(8,128)S(1)} %bitcast.29), channel_id=1, replica_groups=mesh['row'=8,'col'=16] {'row','col'}, dimensions={0} | all-to-all | bytes 1048576 | tf_op jit(solution)/shard_map/all_to_all | solution.py:351
  95.6 2.0 %physical.4 = f32[1024,128]{1,0:T(8,128)S(1)} custom-call(f32[1024,128]{1,0:T(8,128)S(1)} %bitcast.26, bf16[2,256,256]{2,1,0:T(8,128)(2,1)S(1)} %copy-done.5, bf16[2,256,256]{2,1,0:T(8,128)(2,1)S(1)} %copy-done.4, bf16[2,256,256]{2,1,0:T(8,128)(2,1)S(1)} %copy-done.7, bf16[2,256,256]{2,1,0:T(8,128)(2,1)S(1)} %copy-done.9), custom_call_target="tpu_custom_call" | custom-call | tf_op jit(solution)/shard_map/physical/pallas_call | solution.py:339
  97.6 17.6 %all_to_all.43 = f32[128,8,128]{2,1,0:T(8,128)S(1)} all-to-all(f32[128,8,128]{2,1,0:T(8,128)S(1)} %bitcast.27), channel_id=1, replica_groups=mesh['row'=8,'col'=16] {'row','col'}, dimensions={0} | all-to-all | bytes 1048576 | tf_op jit(solution)/shard_map/all_to_all | solution.py:351
  115.3 1.0 spectral_middle.3
  116.2 17.6 %all_to_all.44 = f32[128,8,128]{2,1,0:T(8,128)S(1)} all-to-all(f32[128,8,128]{2,1,0:T(8,128)S(1)} %bitcast.30), channel_id=1, replica_groups=mesh['row'=8,'col'=16] {'row','col'}, dimensions={0} | all-to-all | bytes 1048576 | tf_op jit(solution)/shard_map/all_to_all | solution.py:351
  133.9 2.0 %physical.5 = f32[1024,128]{1,0:T(8,128)S(1)} custom-call(f32[1024,128]{1,0:T(8,128)S(1)} %bitcast.22, bf16[2,256,256]{2,1,0:T(8,128)(2,1)S(1)} %copy-done.5, bf16[2,256,256]{2,1,0:T(8,128)(2,1)S(1)} %copy-done.4, bf16[2,256,256]{2,1,0:T(8,128)(2,1)S(1)} %copy-done.7, bf16[2,256,256]{2,1,0:T(8,128)(2,1)S(1)} %copy-done.9), custom_call_target="tpu_custom_call" | custom-call | tf_op jit(solution)/shard_map/physical/pallas_call | solution.py:339
  135.9 17.6 %all_to_all.45 = f32[128,8,128]{2,1,0:T(8,128)S(1)} all-to-all(f32[128,8,128]{2,1,0:T(8,128)S(1)} %bitcast.23), channel_id=1, replica_groups=mesh['row'=8,'col'=16] {'row','col'}, dimensions={0} | all-to-all | bytes 1048576 | tf_op jit(solution)/shard_map/all_to_all | solution.py:351
  153.6 0.9 spectral_last.1
  154.5 17.6 %all_to_all.46 = f32[128,8,128]{2,1,0:T(8,128)S(1)} all-to-all(f32[128,8,128]{2,1,0:T(8,128)S(1)} %bitcast.20), channel_id=1, replica_groups=mesh['row'=8,'col'=16] {'row','col'}, dimensions={0} | all-to-all | bytes 1048576 | tf_op jit(solution)/shard_map/all_to_all | solution.py:351
  172.2 1.6 last.1
Async XLA Ops:
  0.0 0.9 copy-start.6
  1.0 0.9 copy-start.8
  1.9 1.0 copy-start.10
  5.4 30.4 %all-to-all-start = ((f32[128,16,128]{2,1,0:T(8,128)}), f32[128,16,128]{2,1,0:T(8,128)S(1)}, u32[]{:S(2)}, u32[]{:S(2)}) async-start(f32[128,16,128]{2,1,0:T(8,128)} %bitcast), calls=%async_computation | async-start | bytes 2097152 | tf_op jit(solution)/shard_map/all_to_all | solution.py:351
  35.8 1.0 copy-start
  36.8 0.9 copy-start.2
  37.7 19.5 %copy-start.4 = (bf16[2,256,256]{2,1,0:T(8,128)(2,1)S(1)}, bf16[2,256,256]{2,1,0:T(8,128)(2,1)}, u32[]{:S(2)}) copy-start(bf16[2,256,256]{2,1,0:T(8,128)(2,1)} %constant.17.clone.iz) | copy-start | bytes 786436
  37.7 19.5 %copy-start.5 = (bf16[2,256,256]{2,1,0:T(8,128)(2,1)S(1)}, bf16[2,256,256]{2,1,0:T(8,128)(2,1)}, u32[]{:S(2)}) copy-start(bf16[2,256,256]{2,1,0:T(8,128)(2,1)} %constant.15.clone.iy) | copy-start | bytes 786436
  37.7 19.5 %copy-start.7 = (bf16[2,256,256]{2,1,0:T(8,128)(2,1)S(1)}, bf16[2,256,256]{2,1,0:T(8,128)(2,1)}, u32[]{:S(2)}) copy-start(bf16[2,256,256]{2,1,0:T(8,128)(2,1)} %constant.16.clone.fz) | copy-start | bytes 786436
  37.7 19.5 %copy-start.9 = (bf16[2,256,256]{2,1,0:T(8,128)(2,1)S(1)}, bf16[2,256,256]{2,1,0:T(8,128)(2,1)}, u32[]{:S(2)}) copy-start(bf16[2,256,256]{2,1,0:T(8,128)(2,1)} %constant.14.clone.fy) | copy-start | bytes 786436
  39.4 37.5 %copy-start.1 = (bf16[2,256,256]{2,1,0:T(8,128)(2,1)S(1)}, bf16[2,256,256]{2,1,0:T(8,128)(2,1)}, u32[]{:S(2)}) copy-start(bf16[2,256,256]{2,1,0:T(8,128)(2,1)} %constant.13.clone.ix) | copy-start | bytes 786436
  39.4 37.5 %copy-start.3 = (bf16[2,256,256]{2,1,0:T(8,128)(2,1)S(1)}, bf16[2,256,256]{2,1,0:T(8,128)(2,1)}, u32[]{:S(2)}) copy-start(bf16[2,256,256]{2,1,0:T(8,128)(2,1)} %constant.12.clone.fx) | copy-start | bytes 786436

commit v2 on v1

--- a/solution.py
+++ b/solution.py
@@ -40,7 +40,10 @@
     forward_z = np.concatenate([cosine, minus]).T
     weight = np.where(j == 0, 1.0, 2.0)[:, None] / N
     inverse_z = np.concatenate([cosine * weight, minus * weight])
-    return dict(fx=forward_x, ix=inverse_x, fy=forward_y, iy=inverse_y, fz=forward_z, iz=inverse_z)
+    return forward_z, forward_y, forward_x, inverse_x, inverse_y, inverse_z
+
+
+FZ, FY, FX, IX, IY, IZ = range(6)
 
 
 def split_table(table):
@@ -152,22 +155,44 @@
     send_modes(table_left(fy, half), send, base)
 
 
-def first_kernel(field, fz, fy, send):
+def first_kernel(field_hbm, tabs_hbm, send, factors, tabs, field, sems):
+    def load(source, target, at):
+        return pltpu.make_async_copy(source, target, sems.at[at])
+
+    own = load(field_hbm, field, 0)
+    loads = [load(tabs_hbm.at[k], tabs.at[k], 1 + k) for k in range(6)]
+    own.start()
+    for one in loads:
+        one.start()
+    factor_kernel(factors)
+    own.wait()
+    loads[FZ].wait()
+    loads[FY].wait()
+    fz, fy = tabs.at[FZ], tabs.at[FY]
     for row in range(2):
         values = field[row]
         to_messages(values, send, 4 * row, fz, fy)
         to_messages(reaction(values), send, 8 + 4 * row, fz, fy)
-
-
-def middle_kernel(got, iy, iz, fz, fy, send):
+    for k in (FX, IX, IY, IZ):
+        loads[k].wait()
+
+
+def middle_kernel(got, tabs, send):
+    fz, fy, iy, iz = (tabs.at[k] for k in (FZ, FY, IY, IZ))
     for row in range(2):
         values = from_messages(got, 4 * row, iy, iz)
         to_messages(reaction(values), send, 4 * row, fz, fy)
 
 
-def last_kernel(got, iy, iz, field):
+def last_kernel(got, tabs, field_hbm, field, sems):
+    stores = []
     for row in range(2):
-        field[row] = from_messages(got, 4 * row, iy, iz)
+        field[row] = from_messages(got, 4 * row, tabs.at[IY], tabs.at[IZ])
+        one = pltpu.make_async_copy(field.at[row], field_hbm.at[row], sems.at[row])
+        one.start()
+        stores.append(one)
+    for one in stores:
+        one.wait()
 
 
 def special_lane(slot):
@@ -229,7 +254,8 @@
             yield 2 * half + part, half, part
 
 
-def spectral_first(got, factors, fx, ix, send, keep, base, total):
+def spectral_first(got, factors, tabs, send, keep, base, total):
+    fx, ix = tabs.at[FX], tabs.at[IX]
     for slot in range(2):
         state = spectrum_of(got, slot, fx)
         react = spectrum_of(got, slot, fx, field=1)
@@ -248,7 +274,8 @@
         spectrum_to(nexts, slot, ix, send)
 
 
-def spectral_middle(got, factors, kept, total, fx, ix, send, total_out, *, twice):
+def spectral_middle(got, factors, kept, total, tabs, send, total_out, *, twice):
+    fx, ix = tabs.at[FX], tabs.at[IX]
     for slot in range(2):
         react = spectrum_of(got, slot, fx)
         nexts = []
@@ -262,7 +289,8 @@
         spectrum_to(nexts, slot, ix, send)
 
 
-def spectral_last(got, factors, total, fx, ix, send):
+def spectral_last(got, factors, total, tabs, send):
+    fx, ix = tabs.at[FX], tabs.at[IX]
     for slot in range(2):
         react = spectrum_of(got, slot, fx)
         nexts = []
@@ -333,14 +361,18 @@
     return jax.ShapeDtypeStruct(dims, F32)
 
 
-def call(kernel, outs, *args, name):
-    vmem = pl.BlockSpec(memory_space=pltpu.VMEM)
+VMEM = pl.BlockSpec(memory_space=pltpu.VMEM)
+HBM = pl.BlockSpec(memory_space=pltpu.HBM)
+
+
+def call(kernel, outs, *args, name, ins=VMEM, into=VMEM, scratch=()):
     single = not isinstance(outs, tuple)
     return pl.pallas_call(
         kernel,
         out_shape=outs,
-        in_specs=[vmem] * len(args),
-        out_specs=vmem if single else tuple(vmem for _ in outs),
+        in_specs=[ins] * len(args),
+        out_specs=into if single else tuple(into for _ in outs),
+        scratch_shapes=scratch,
         compiler_params=pltpu.CompilerParams(vmem_limit_bytes=16 << 20),
         name=name,
     )(*args)
@@ -353,37 +385,50 @@
 
 
 def body(tabs, field):
-    fx, ix, fy, iy, fz, iz = (tabs[k] for k in ("fx", "ix", "fy", "iy", "fz", "iz"))
     message = shape(8 * H, H)
     spectrum = shape(8, H, H)
-    factors = call(factor_kernel, shape(6, 6, H, H), name="factors")
-    send = call(first_kernel, shape(16 * H, H), field, fz, fy, name="first")
+    send, factors, tabs = call(
+        first_kernel,
+        (shape(16 * H, H), shape(6, 6, H, H), jax.ShapeDtypeStruct(tabs.shape, BF16)),
+        pltpu.with_memory_space_constraint(field, pltpu.HBM),
+        pltpu.with_memory_space_constraint(tabs, pltpu.HBM),
+        name="first",
+        ins=HBM,
+        scratch=[pltpu.VMEM(field.shape, F32), pltpu.SemaphoreType.DMA((7,))],
+    )
     got = move(send)
     send, keep, base, total = call(
-        spectral_first, (message, spectrum, spectrum, spectrum), got, factors, fx, ix, name="spectral_first"
+        spectral_first, (message, spectrum, spectrum, spectrum), got, factors, tabs, name="spectral_first"
     )
 
     def physical(send):
-        return move(call(middle_kernel, message, move(send), iy, iz, fz, fy, name="physical"))
+        return move(call(middle_kernel, message, move(send), tabs, name="physical"))
 
     for kept, twice in ((keep, False), (base, True)):
         got = physical(send)
         send, total = call(
             functools.partial(spectral_middle, twice=twice),
             (message, spectrum),
-            got, factors, kept, total, fx, ix,
+            got, factors, kept, total, tabs,
             name="spectral_middle",
         )
     got = physical(send)
-    send = call(spectral_last, message, got, factors, total, fx, ix, name="spectral_last")
-    return call(last_kernel, shape(2, N, N), move(send), iy, iz, name="last")
+    send = call(spectral_last, message, got, factors, total, tabs, name="spectral_last")
+    return call(
+        last_kernel,
+        shape(*field.shape),
+        move(send), tabs,
+        name="last",
+        into=HBM,
+        scratch=[pltpu.VMEM(field.shape, F32), pltpu.SemaphoreType.DMA((2,))],
+    )
 
 
 def solution(mesh):
-    tabs = {k: split_table(v) for k, v in tables().items()}
+    tabs = np.stack([split_table(t) for t in tables()])
     placed = P(BOTH, None, None)
 
     def run(initial_field):
-        return body({k: jnp.asarray(v) for k, v in tabs.items()}, initial_field)
+        return body(jnp.asarray(tabs), initial_field)
 
     return jax.shard_map(run, mesh=mesh, in_specs=(placed,), out_specs=placed, check_vma=False)

time: 174 us -> 169 us (0.971)
  blocking collectives: 124 us -> 154 us
  waiting for transfers between devices: 17.9 us -> 0 us
  starting transfers between devices: 11.5 us -> 0 us
  local copies, waits for them, and re-layouts: 4.87 us -> 0 us
    all_to_all x7 -> x8, blocking collectives: 124 us -> 154 us  [move(): out = lax.all_to_all(tiles, BOTH, split_axis=0, concat_axis=0, tiled=True)]
    all_to_all x1 -> x0, waiting for transfers between devices: 17.9 us -> none  [move(): out = lax.all_to_all(tiles, BOTH, split_axis=0, concat_axis=0, tiled=True)]
    all_to_all x1 -> x0, starting transfers between devices: 11.5 us -> none  [move(): out = lax.all_to_all(tiles, BOTH, split_axis=0, concat_axis=0, tiled=True)]
    unnamed x22 -> x0, local copies, waits for them, and re-layouts: 4.87 us -> none
    pallas_call x10 -> x9, Pallas kernels: 15.8 us -> 14.9 us  [call(): pl.pallas_call(kernel, out_shape=outs, in_specs=[ins] * len(args), out_sp...]
  transfers between devices with their start and end apart: 1 -> 0, of which waited for: 1 -> 0; matrix products, arithmetic and copies ran while one was open for 0% -> 0% of each run, Pallas kernels for 1% -> 0%
where the time goes in v2:
time: 169 us
  blocking collectives  154 us (91%)
  Pallas kernels  14.9 us (9%)
    all_to_all x8, blocking collectives, move(): out = lax.all_to_all(tiles, BOTH, split_axis=0, concat_axis=0, tiled=True)  154 us
    pallas_call x9, Pallas kernels, call(): pl.pallas_call(kernel, out_shape=outs, in_specs=[ins] * len(args), out_sp...  14.9 us

profile of v2, /device:TPU:1, one launch (start us, length us, event | category | flops | bytes accessed | tf_op | source)
XLA Modules:
  0.0 169.0 jit_solution(2058597042616209430)
XLA Ops:
  0.0 2.7 %first.1 = (f32[2048,128]{1,0:T(8,128)S(1)}, f32[6,6,128,128]{3,2,1,0:T(8,128)S(1)}, bf16[6,2,256,256]{3,2,1,0:T(8,128)(2,1)S(1)}) custom-call(f32[2,256,256]{2,1,0:T(8,128)} %field_hbm.1, bf16[6,2,256,256]{3,2,1,0:T(8,128)(2,1)} %constant.2.clone.tabs_hbm), custom_call_target="tpu_custom_call" | custom-call | tf_op jit(solution)/shard_map/first/pallas_call | solution.py:370
  2.7 30.2 %all_to_all.40 = f32[128,16,128]{2,1,0:T(8,128)S(1)} all-to-all(f32[128,16,128]{2,1,0:T(8,128)S(1)} %bitcast.28), channel_id=1, replica_groups=mesh['row'=8,'col'=16] {'row','col'}, dimensions={0} | all-to-all | bytes 2097152 | tf_op jit(solution)/shard_map/all_to_all | solution.py:383
  33.0 1.7 spectral_first.1
  34.6 17.7 %all_to_all.41 = f32[128,8,128]{2,1,0:T(8,128)S(1)} all-to-all(f32[128,8,128]{2,1,0:T(8,128)S(1)} %bitcast.29), channel_id=1, replica_groups=mesh['row'=8,'col'=16] {'row','col'}, dimensions={0} | all-to-all | bytes 1048576 | tf_op jit(solution)/shard_map/all_to_all | solution.py:383
  52.4 2.0 %physical.3 = f32[1024,128]{1,0:T(8,128)S(1)} custom-call(f32[1024,128]{1,0:T(8,128)S(1)} %bitcast.18, bf16[6,2,256,256]{3,2,1,0:T(8,128)(2,1)S(1)} %get-tuple-element.18.tabs), custom_call_target="tpu_custom_call" | custom-call | tf_op jit(solution)/shard_map/physical/pallas_call | solution.py:370
  54.4 17.6 %all_to_all.42 = f32[128,8,128]{2,1,0:T(8,128)S(1)} all-to-all(f32[128,8,128]{2,1,0:T(8,128)S(1)} %bitcast.19), channel_id=1, replica_groups=mesh['row'=8,'col'=16] {'row','col'}, dimensions={0} | all-to-all | bytes 1048576 | tf_op jit(solution)/shard_map/all_to_all | solution.py:383
  72.1 1.0 spectral_middle.2
  73.0 17.6 %all_to_all.43 = f32[128,8,128]{2,1,0:T(8,128)S(1)} all-to-all(f32[128,8,128]{2,1,0:T(8,128)S(1)} %bitcast.30), channel_id=1, replica_groups=mesh['row'=8,'col'=16] {'row','col'}, dimensions={0} | all-to-all | bytes 1048576 | tf_op jit(solution)/shard_map/all_to_all | solution.py:383
  90.7 2.0 %physical.4 = f32[1024,128]{1,0:T(8,128)S(1)} custom-call(f32[1024,128]{1,0:T(8,128)S(1)} %bitcast.20, bf16[6,2,256,256]{3,2,1,0:T(8,128)(2,1)S(1)} %get-tuple-element.18.tabs), custom_call_target="tpu_custom_call" | custom-call | tf_op jit(solution)/shard_map/physical/pallas_call | solution.py:370
  92.7 17.6 %all_to_all.44 = f32[128,8,128]{2,1,0:T(8,128)S(1)} all-to-all(f32[128,8,128]{2,1,0:T(8,128)S(1)} %bitcast.21), channel_id=1, replica_groups=mesh['row'=8,'col'=16] {'row','col'}, dimensions={0} | all-to-all | bytes 1048576 | tf_op jit(solution)/shard_map/all_to_all | solution.py:383
  110.4 1.0 spectral_middle.3
  111.4 17.6 %all_to_all.45 = f32[128,8,128]{2,1,0:T(8,128)S(1)} all-to-all(f32[128,8,128]{2,1,0:T(8,128)S(1)} %bitcast.31), channel_id=1, replica_groups=mesh['row'=8,'col'=16] {'row','col'}, dimensions={0} | all-to-all | bytes 1048576 | tf_op jit(solution)/shard_map/all_to_all | solution.py:383
  129.0 2.0 %physical.5 = f32[1024,128]{1,0:T(8,128)S(1)} custom-call(f32[1024,128]{1,0:T(8,128)S(1)} %bitcast.22, bf16[6,2,256,256]{3,2,1,0:T(8,128)(2,1)S(1)} %get-tuple-element.18.tabs), custom_call_target="tpu_custom_call" | custom-call | tf_op jit(solution)/shard_map/physical/pallas_call | solution.py:370
  131.1 17.6 %all_to_all.46 = f32[128,8,128]{2,1,0:T(8,128)S(1)} all-to-all(f32[128,8,128]{2,1,0:T(8,128)S(1)} %bitcast.23), channel_id=1, replica_groups=mesh['row'=8,'col'=16] {'row','col'}, dimensions={0} | all-to-all | bytes 1048576 | tf_op jit(solution)/shard_map/all_to_all | solution.py:383
  148.7 0.9 spectral_last.1
  149.6 17.6 %all_to_all.47 = f32[128,8,128]{2,1,0:T(8,128)S(1)} all-to-all(f32[128,8,128]{2,1,0:T(8,128)S(1)} %bitcast.27), channel_id=1, replica_groups=mesh['row'=8,'col'=16] {'row','col'}, dimensions={0} | all-to-all | bytes 1048576 | tf_op jit(solution)/shard_map/all_to_all | solution.py:383
  167.3 1.6 last.1

commit v3 on v2

--- a/solution.py
+++ b/solution.py
@@ -62,9 +62,10 @@
     return jnp.dot(left, right, preferred_element_type=F32)
 
 
-def table_left(table, values):
-    high, low = split(values)
-    return dot(table[0], high) + (dot(table[0], low) + dot(table[1], high))
+def table_left(table, parts, at=0, count=N):
+    high, low = parts
+    top, bottom = table[0, pl.ds(at, count), :], table[1, pl.ds(at, count), :]
+    return dot(top, high) + (dot(top, low) + dot(bottom, high))
 
 
 def table_right(values, table):
@@ -144,15 +145,24 @@
     return joined(pre, pim, mre, mim)
 
 
-def from_messages(got, base, iy, iz):
-    modes = got_modes(got, base)
-    half = table_left(iy, modes)
-    return table_right(half, iz)
-
-
-def to_messages(values, send, base, fz, fy):
-    half = table_right(values, fz)
-    send_modes(table_left(fy, half), send, base)
+ROWS = range(2)
+HALVES = range(2)
+PIECES = [(row, half) for row in ROWS for half in HALVES]
+
+
+def from_messages(got, iy, iz):
+    modes = [split(got_modes(got, 4 * row)) for row in ROWS]
+    parts = [table_left(iy, modes[row], H * half, H) for row, half in PIECES]
+    return [table_right(part, iz) for part in parts]
+
+
+def to_messages(fields, send, fz, fy):
+    parts = [[table_right(piece, fz) for piece in field] for field in fields]
+    whole = [
+        split(jnp.concatenate(part[2 * row : 2 * row + 2], axis=0)) for part in parts for row in ROWS
+    ]
+    for slot, modes in enumerate(whole):
+        send_modes(table_left(fy, modes), send, 4 * slot)
 
 
 def first_kernel(field_hbm, tabs_hbm, send, factors, tabs, field, sems):
@@ -168,27 +178,24 @@
     own.wait()
     loads[FZ].wait()
     loads[FY].wait()
-    fz, fy = tabs.at[FZ], tabs.at[FY]
-    for row in range(2):
-        values = field[row]
-        to_messages(values, send, 4 * row, fz, fy)
-        to_messages(reaction(values), send, 8 + 4 * row, fz, fy)
+    pieces = [field[row, pl.ds(H * half, H), :] for row, half in PIECES]
+    to_messages([pieces, [reaction(v) for v in pieces]], send, tabs.at[FZ], tabs.at[FY])
     for k in (FX, IX, IY, IZ):
         loads[k].wait()
 
 
 def middle_kernel(got, tabs, send):
-    fz, fy, iy, iz = (tabs.at[k] for k in (FZ, FY, IY, IZ))
-    for row in range(2):
-        values = from_messages(got, 4 * row, iy, iz)
-        to_messages(reaction(values), send, 4 * row, fz, fy)
+    pieces = from_messages(got, tabs.at[IY], tabs.at[IZ])
+    to_messages([[reaction(v) for v in pieces]], send, tabs.at[FZ], tabs.at[FY])
 
 
 def last_kernel(got, tabs, field_hbm, field, sems):
     stores = []
-    for row in range(2):
-        field[row] = from_messages(got, 4 * row, tabs.at[IY], tabs.at[IZ])
-        one = pltpu.make_async_copy(field.at[row], field_hbm.at[row], sems.at[row])
+    pieces = from_messages(got, tabs.at[IY], tabs.at[IZ])
+    for k, (row, half) in enumerate(PIECES):
+        at = pl.ds(H * half, H)
+        field[row, at, :] = pieces[k]
+        one = pltpu.make_async_copy(field.at[row, at], field_hbm.at[row, at], sems.at[k])
         one.start()
         stores.append(one)
     for one in stores:
@@ -203,10 +210,14 @@
     return (lane == 0) & (grid_of(0) != 0)
 
 
-def spectrum_of(got, slot, fx, field=0):
+def column_of(got, slot, field=0):
     at = 8 * field + 2 * slot
     column = joined(*(tile_rows(got, at + k) for k in (0, 1, 4, 5)))
-    cre, cim, sre, sim = quarters(table_left(fx, column))
+    return split(column)
+
+
+def modes_of(whole, slot):
+    cre, cim, sre, sim = quarters(whole)
     row0 = grid_of(0) == 0
     tre = jnp.where(row0, cre, cre + sim)
     tim = jnp.where(row0, cim, cim - sre)
@@ -221,7 +232,14 @@
     return tre, tim, bre, bim
 
 
-def spectrum_to(parts, slot, ix, send):
+def spectra_of(got, fx, fields=1):
+    keys = [(slot, field) for slot in range(2) for field in range(fields)]
+    columns = [column_of(got, *key) for key in keys]
+    wholes = [table_left(fx, column) for column in columns]
+    return {key: modes_of(whole, key[0]) for key, whole in zip(keys, wholes)}
+
+
+def operand_of(parts, slot):
     tre, tim, bre, bim = parts
     row0 = grid_of(0) == 0
     pre = jnp.where(row0, tre, tre + bre)
@@ -234,12 +252,16 @@
         pim = jnp.where(special, 2.0 * bre, pim)
         mre = jnp.where(special, -2.0 * tim, mre)
         mim = jnp.where(special, -2.0 * bim, mim)
-    out = table_left(ix, joined(pre, pim, mre, mim))
-    a, b, c, d = quarters(out)
-    put_rows(send, 2 * slot, a)
-    put_rows(send, 2 * slot + 1, b)
-    put_rows(send, 2 * slot + 4, c)
-    put_rows(send, 2 * slot + 5, d)
+    return split(joined(pre, pim, mre, mim))
+
+
+def spectra_to(nexts, ix, send):
+    operands = [operand_of(parts, slot) for slot, parts in enumerate(nexts)]
+    for slot, operand in enumerate(operands):
+        for row in ROWS:
+            out = table_left(ix, operand, H * row, H)
+            put_rows(send, 4 * row + 2 * slot, out[:, :H])
+            put_rows(send, 4 * row + 2 * slot + 1, out[:, H:])
 
 
 def plane_of(slot, half, part):
@@ -255,11 +277,10 @@
 
 
 def spectral_first(got, factors, tabs, send, keep, base, total):
-    fx, ix = tabs.at[FX], tabs.at[IX]
+    spectra = spectra_of(got, tabs.at[FX], 2)
+    nexts = [[], []]
     for slot in range(2):
-        state = spectrum_of(got, slot, fx)
-        react = spectrum_of(got, slot, fx, field=1)
-        nexts = []
+        state, react = spectra[slot, 0], spectra[slot, 1]
         for k, half, part in each_part():
             plane = plane_of(slot, half, part)
             e_half = factors[0, plane]
@@ -270,34 +291,34 @@
             keep[4 * slot + k] = kept
             base[4 * slot + k] = e_half * first - turn
             total[4 * slot + k] = factors[2, plane] * state[k] + factors[3, plane] * react[k]
-            nexts.append(first)
-        spectrum_to(nexts, slot, ix, send)
+            nexts[slot].append(first)
+    spectra_to(nexts, tabs.at[IX], send)
 
 
 def spectral_middle(got, factors, kept, total, tabs, send, total_out, *, twice):
-    fx, ix = tabs.at[FX], tabs.at[IX]
+    spectra = spectra_of(got, tabs.at[FX])
+    nexts = [[], []]
     for slot in range(2):
-        react = spectrum_of(got, slot, fx)
-        nexts = []
+        react = spectra[slot, 0]
         for k, half, part in each_part():
             plane = plane_of(slot, half, part)
             turn = factors[1, plane] * react[k]
             if twice:
                 turn = 2.0 * turn
-            nexts.append(kept[4 * slot + k] + turn)
+            nexts[slot].append(kept[4 * slot + k] + turn)
             total_out[4 * slot + k] = total[4 * slot + k] + 2.0 * factors[4, plane] * react[k]
-        spectrum_to(nexts, slot, ix, send)
+    spectra_to(nexts, tabs.at[IX], send)
 
 
 def spectral_last(got, factors, total, tabs, send):
-    fx, ix = tabs.at[FX], tabs.at[IX]
+    spectra = spectra_of(got, tabs.at[FX])
+    nexts = [[], []]
     for slot in range(2):
-        react = spectrum_of(got, slot, fx)
-        nexts = []
+        react = spectra[slot, 0]
         for k, half, part in each_part():
             plane = plane_of(slot, half, part)
-            nexts.append(total[4 * slot + k] + factors[5, plane] * react[k])
-        spectrum_to(nexts, slot, ix, send)
+            nexts[slot].append(total[4 * slot + k] + factors[5, plane] * react[k])
+    spectra_to(nexts, tabs.at[IX], send)
 
 
 def phi_values(argument, degrees):
@@ -420,7 +441,7 @@
         move(send), tabs,
         name="last",
         into=HBM,
-        scratch=[pltpu.VMEM(field.shape, F32), pltpu.SemaphoreType.DMA((2,))],
+        scratch=[pltpu.VMEM(field.shape, F32), pltpu.SemaphoreType.DMA((4,))],
     )
 
 

time: 169 us -> 166 us (0.982)
  Pallas kernels: 14.9 us -> 11.6 us
    pallas_call x9, Pallas kernels: 14.9 us -> 11.6 us  [call(): pl.pallas_call(kernel, out_shape=outs, in_specs=[ins] * len(args), out_sp...]
where the time goes in v3:
time: 166 us
  blocking collectives  154 us (93%)
  Pallas kernels  11.6 us (7%)
    all_to_all x8, blocking collectives, move(): out = lax.all_to_all(tiles, BOTH, split_axis=0, concat_axis=0, tiled=True)  154 us
    pallas_call x9, Pallas kernels, call(): pl.pallas_call(kernel, out_shape=outs, in_specs=[ins] * len(args), out_sp...  11.6 us

profile of v3, /device:TPU:1, one launch (start us, length us, event | category | flops | bytes accessed | tf_op | source)
XLA Modules:
  0.0 165.7 jit_solution(14078353668479080885)
XLA Ops:
  0.0 2.5 %first.1 = (f32[2048,128]{1,0:T(8,128)S(1)}, f32[6,6,128,128]{3,2,1,0:T(8,128)S(1)}, bf16[6,2,256,256]{3,2,1,0:T(8,128)(2,1)S(1)}) custom-call(f32[2,256,256]{2,1,0:T(8,128)} %field_hbm.1, bf16[6,2,256,256]{3,2,1,0:T(8,128)(2,1)} %constant.2.clone.tabs_hbm), custom_call_target="tpu_custom_call" | custom-call | tf_op jit(solution)/shard_map/first/pallas_call | solution.py:391
  2.5 30.2 %all_to_all.40 = f32[128,16,128]{2,1,0:T(8,128)S(1)} all-to-all(f32[128,16,128]{2,1,0:T(8,128)S(1)} %bitcast.28), channel_id=1, replica_groups=mesh['row'=8,'col'=16] {'row','col'}, dimensions={0} | all-to-all | bytes 2097152 | tf_op jit(solution)/shard_map/all_to_all | solution.py:404
  32.7 1.2 spectral_first.1
  34.0 17.7 %all_to_all.41 = f32[128,8,128]{2,1,0:T(8,128)S(1)} all-to-all(f32[128,8,128]{2,1,0:T(8,128)S(1)} %bitcast.29), channel_id=1, replica_groups=mesh['row'=8,'col'=16] {'row','col'}, dimensions={0} | all-to-all | bytes 1048576 | tf_op jit(solution)/shard_map/all_to_all | solution.py:404
  51.7 1.2 physical.3
  52.9 17.6 %all_to_all.42 = f32[128,8,128]{2,1,0:T(8,128)S(1)} all-to-all(f32[128,8,128]{2,1,0:T(8,128)S(1)} %bitcast.19), channel_id=1, replica_groups=mesh['row'=8,'col'=16] {'row','col'}, dimensions={0} | all-to-all | bytes 1048576 | tf_op jit(solution)/shard_map/all_to_all | solution.py:404
  70.6 1.0 spectral_middle.2
  71.5 17.6 %all_to_all.43 = f32[128,8,128]{2,1,0:T(8,128)S(1)} all-to-all(f32[128,8,128]{2,1,0:T(8,128)S(1)} %bitcast.30), channel_id=1, replica_groups=mesh['row'=8,'col'=16] {'row','col'}, dimensions={0} | all-to-all | bytes 1048576 | tf_op jit(solution)/shard_map/all_to_all | solution.py:404
  89.2 1.2 physical.4
  90.4 17.6 %all_to_all.44 = f32[128,8,128]{2,1,0:T(8,128)S(1)} all-to-all(f32[128,8,128]{2,1,0:T(8,128)S(1)} %bitcast.21), channel_id=1, replica_groups=mesh['row'=8,'col'=16] {'row','col'}, dimensions={0} | all-to-all | bytes 1048576 | tf_op jit(solution)/shard_map/all_to_all | solution.py:404
  108.0 1.0 spectral_middle.3
  109.1 17.6 %all_to_all.45 = f32[128,8,128]{2,1,0:T(8,128)S(1)} all-to-all(f32[128,8,128]{2,1,0:T(8,128)S(1)} %bitcast.31), channel_id=1, replica_groups=mesh['row'=8,'col'=16] {'row','col'}, dimensions={0} | all-to-all | bytes 1048576 | tf_op jit(solution)/shard_map/all_to_all | solution.py:404
  126.7 1.2 physical.5
  127.9 17.6 %all_to_all.46 = f32[128,8,128]{2,1,0:T(8,128)S(1)} all-to-all(f32[128,8,128]{2,1,0:T(8,128)S(1)} %bitcast.23), channel_id=1, replica_groups=mesh['row'=8,'col'=16] {'row','col'}, dimensions={0} | all-to-all | bytes 1048576 | tf_op jit(solution)/shard_map/all_to_all | solution.py:404
  145.6 0.9 spectral_last.1
  146.5 17.6 %all_to_all.47 = f32[128,8,128]{2,1,0:T(8,128)S(1)} all-to-all(f32[128,8,128]{2,1,0:T(8,128)S(1)} %bitcast.27), channel_id=1, replica_groups=mesh['row'=8,'col'=16] {'row','col'}, dimensions={0} | all-to-all | bytes 1048576 | tf_op jit(solution)/shard_map/all_to_all | solution.py:404
  164.1 1.4 last.1

commit v4 on v3

--- a/solution.py
+++ b/solution.py
@@ -16,6 +16,7 @@
 
 N = 256
 H = 128
+Q = 64
 BOTH = ("row", "col")
 F32 = jnp.float32
 BF16 = jnp.bfloat16
@@ -33,8 +34,10 @@
     forward_y = np.concatenate([cosine, sine_alt])
     inverse_y = forward_y.T / N
     order = np.concatenate([np.arange(0, N, 2), np.arange(1, N, 2)])
+    pieces = np.arange(N).reshape(2, 2, Q).transpose(1, 0, 2).reshape(N)
+    inverse_x = inverse_y[order]
+    forward_y = forward_y[pieces]
     forward_x = forward_y[:, order]
-    inverse_x = inverse_y[order]
     minus = -sine
     minus[0] = alternate
     forward_z = np.concatenate([cosine, minus]).T
@@ -77,8 +80,20 @@
     return lax.broadcasted_iota(jnp.int32, (H, H), axis)
 
 
+def piece_grid(axis):
+    return lax.broadcasted_iota(jnp.int32, (Q, H), axis)
+
+
+def first_row(piece):
+    return None if piece else piece_grid(0) == 0
+
+
+def pick(mask, chosen, other):
+    return other if mask is None else jnp.where(mask, chosen, other)
+
+
 def quarters(whole):
-    return whole[:H, :H], whole[:H, H:], whole[H:, :H], whole[H:, H:]
+    return whole[:Q, :H], whole[:Q, H:], whole[Q:, :H], whole[Q:, H:]
 
 
 def joined(top_left, top_right, bottom_left, bottom_right):
@@ -95,32 +110,28 @@
     return ref[pl.ds(slot, H, stride=ref.shape[0] // H), :]
 
 
-def put_rows(ref, slot, values):
-    ref[pl.ds(slot, H, stride=ref.shape[0] // H), :] = values
+def put_rows(ref, slot, values, at=0):
+    stride = ref.shape[0] // H
+    ref[pl.ds(slot + stride * at, values.shape[0], stride=stride), :] = values
 
 
 def reaction(values):
     return quadratic * values * values - values * values * values
 
 
-def send_modes(whole, send, base):
+def send_modes(whole, piece, send, base):
     cre, cim, sre, sim = quarters(whole)
-    lane0 = grid_of(1) == 0
-    row0 = grid_of(0) == 0
-    corner = lane0 & row0
-    o0re = jnp.where(lane0 | row0, cre, cre + sim)
-    o0im = jnp.where(lane0, -sre, cim - sre)
-    o0im = jnp.where(row0, cim, o0im)
-    o0im = jnp.where(corner, sim, o0im)
-    o1re = jnp.where(row0, sre, cre - sim)
-    o1re = jnp.where(lane0, cim, o1re)
-    o1im = jnp.where(lane0, -sim, cim + sre)
-    o1im = jnp.where(row0, sim, o1im)
-    o1im = jnp.where(corner, sre, o1im)
-    put_rows(send, base + 0, o0re)
-    put_rows(send, base + 1, o0im)
-    put_rows(send, base + 2, o1re)
-    put_rows(send, base + 3, o1im)
+    lane0 = piece_grid(1) == 0
+    row0 = first_row(piece)
+    corner = None if row0 is None else lane0 & row0
+    o0re = jnp.where(lane0 if row0 is None else lane0 | row0, cre, cre + sim)
+    o0im = pick(row0, cim, jnp.where(lane0, -sre, cim - sre))
+    o0im = pick(corner, sim, o0im)
+    o1re = jnp.where(lane0, cim, pick(row0, sre, cre - sim))
+    o1im = pick(row0, sim, jnp.where(lane0, -sim, cim + sre))
+    o1im = pick(corner, sre, o1im)
+    for k, values in enumerate((o0re, o0im, o1re, o1im)):
+        put_rows(send, base + k, values, Q * piece)
 
 
 def got_modes(got, base):
@@ -162,7 +173,8 @@
         split(jnp.concatenate(part[2 * row : 2 * row + 2], axis=0)) for part in parts for row in ROWS
     ]
     for slot, modes in enumerate(whole):
-        send_modes(table_left(fy, modes), send, 4 * slot)
+        for piece in range(2):
+            send_modes(table_left(fy, modes, H * piece, H), piece, send, 4 * slot)
 
 
 def first_kernel(field_hbm, tabs_hbm, send, factors, tabs, field, sems):
@@ -171,13 +183,13 @@
 
     own = load(field_hbm, field, 0)
     loads = [load(tabs_hbm.at[k], tabs.at[k], 1 + k) for k in range(6)]
-    own.start()
-    for one in loads:
+    for one in (own, loads[FZ], loads[FY]):
         one.start()
     factor_kernel(factors)
-    own.wait()
-    loads[FZ].wait()
-    loads[FY].wait()
+    for one in (own, loads[FZ], loads[FY]):
+        one.wait()
+    for k in (FX, IX, IY, IZ):
+        loads[k].start()
     pieces = [field[row, pl.ds(H * half, H), :] for row, half in PIECES]
     to_messages([pieces, [reaction(v) for v in pieces]], send, tabs.at[FZ], tabs.at[FY])
     for k in (FX, IX, IY, IZ):
@@ -202,12 +214,12 @@
         one.wait()
 
 
-def special_lane(slot):
+def special_lane(slot, row0):
     if slot:
         return None
     device = lax.axis_index(BOTH)
-    lane = grid_of(1) + jnp.where(device == 0, 0, H)
-    return (lane == 0) & (grid_of(0) != 0)
+    lane = piece_grid(1) + jnp.where(device == 0, 0, H) == 0
+    return lane if row0 is None else lane & ~row0
 
 
 def column_of(got, slot, field=0):
@@ -216,48 +228,52 @@
     return split(column)
 
 
-def modes_of(whole, slot):
+def modes_of(whole, slot, piece):
     cre, cim, sre, sim = quarters(whole)
-    row0 = grid_of(0) == 0
-    tre = jnp.where(row0, cre, cre + sim)
-    tim = jnp.where(row0, cim, cim - sre)
-    bre = jnp.where(row0, sre, cre - sim)
-    bim = jnp.where(row0, sim, cim + sre)
-    special = special_lane(slot)
-    if special is not None:
-        tre = jnp.where(special, cre, tre)
-        tim = jnp.where(special, -sre, tim)
-        bre = jnp.where(special, cim, bre)
-        bim = jnp.where(special, -sim, bim)
+    row0 = first_row(piece)
+    special = special_lane(slot, row0)
+    tre = pick(special, cre, pick(row0, cre, cre + sim))
+    tim = pick(special, -sre, pick(row0, cim, cim - sre))
+    bre = pick(special, cim, pick(row0, sre, cre - sim))
+    bim = pick(special, -sim, pick(row0, sim, cim + sre))
     return tre, tim, bre, bim
+
+
+PARTS = [(slot, piece) for slot in range(2) for piece in range(2)]
 
 
 def spectra_of(got, fx, fields=1):
     keys = [(slot, field) for slot in range(2) for field in range(fields)]
-    columns = [column_of(got, *key) for key in keys]
-    wholes = [table_left(fx, column) for column in columns]
-    return {key: modes_of(whole, key[0]) for key, whole in zip(keys, wholes)}
-
-
-def operand_of(parts, slot):
+    columns = {key: column_of(got, *key) for key in keys}
+    return {
+        (slot, piece): [
+            modes_of(table_left(fx, columns[slot, field], H * piece, H), slot, piece)
+            for field in range(fields)
+        ]
+        for slot, piece in PARTS
+    }
+
+
+def operand_of(parts, slot, piece):
     tre, tim, bre, bim = parts
-    row0 = grid_of(0) == 0
-    pre = jnp.where(row0, tre, tre + bre)
-    pim = jnp.where(row0, tim, tim + bim)
-    mre = jnp.where(row0, bre, bim - tim)
-    mim = jnp.where(row0, bim, tre - bre)
-    special = special_lane(slot)
-    if special is not None:
-        pre = jnp.where(special, 2.0 * tre, pre)
-        pim = jnp.where(special, 2.0 * bre, pim)
-        mre = jnp.where(special, -2.0 * tim, mre)
-        mim = jnp.where(special, -2.0 * bim, mim)
-    return split(joined(pre, pim, mre, mim))
+    row0 = first_row(piece)
+    special = special_lane(slot, row0)
+    pre = pick(special, 2.0 * tre, pick(row0, tre, tre + bre))
+    pim = pick(special, 2.0 * bre, pick(row0, tim, tim + bim))
+    mre = pick(special, -2.0 * tim, pick(row0, bre, bim - tim))
+    mim = pick(special, -2.0 * bim, pick(row0, bim, tre - bre))
+    plus = split(jnp.concatenate([pre, pim], axis=1))
+    minus = split(jnp.concatenate([mre, mim], axis=1))
+    return plus, minus
 
 
 def spectra_to(nexts, ix, send):
-    operands = [operand_of(parts, slot) for slot, parts in enumerate(nexts)]
-    for slot, operand in enumerate(operands):
+    sides = {key: operand_of(nexts[key], *key) for key in PARTS}
+    for slot in range(2):
+        one, two = sides[slot, 0], sides[slot, 1]
+        operand = [
+            jnp.concatenate([one[0][k], two[0][k], one[1][k], two[1][k]], axis=0) for k in range(2)
+        ]
         for row in ROWS:
             out = table_left(ix, operand, H * row, H)
             put_rows(send, 4 * row + 2 * slot, out[:, :H])
@@ -270,112 +286,119 @@
     return (4 if part else 0) + half
 
 
-def each_part():
+def each_part(slot, piece):
+    rows = pl.ds(Q * piece, Q)
     for half in range(2):
         for part in range(2):
-            yield 2 * half + part, half, part
+            k = 2 * half + part
+            yield k, (4 * slot + k, rows), (plane_of(slot, half, part), rows)
 
 
 def spectral_first(got, factors, tabs, send, keep, base, total):
     spectra = spectra_of(got, tabs.at[FX], 2)
-    nexts = [[], []]
-    for slot in range(2):
-        state, react = spectra[slot, 0], spectra[slot, 1]
-        for k, half, part in each_part():
-            plane = plane_of(slot, half, part)
-            e_half = factors[0, plane]
-            q_half = factors[1, plane]
+    nexts = {}
+    for key in PARTS:
+        state, react = spectra[key]
+        nexts[key] = []
+        for k, own, plane in each_part(*key):
+            e_half = factors[0, *plane]
+            q_half = factors[1, *plane]
             kept = e_half * state[k]
             turn = q_half * react[k]
             first = kept + turn
-            keep[4 * slot + k] = kept
-            base[4 * slot + k] = e_half * first - turn
-            total[4 * slot + k] = factors[2, plane] * state[k] + factors[3, plane] * react[k]
-            nexts[slot].append(first)
+            keep[own] = kept
+            base[own] = e_half * first - turn
+            total[own] = factors[2, *plane] * state[k] + factors[3, *plane] * react[k]
+            nexts[key].append(first)
     spectra_to(nexts, tabs.at[IX], send)
 
 
 def spectral_middle(got, factors, kept, total, tabs, send, total_out, *, twice):
     spectra = spectra_of(got, tabs.at[FX])
-    nexts = [[], []]
-    for slot in range(2):
-        react = spectra[slot, 0]
-        for k, half, part in each_part():
-            plane = plane_of(slot, half, part)
-            turn = factors[1, plane] * react[k]
+    nexts = {}
+    for key in PARTS:
+        (react,) = spectra[key]
+        nexts[key] = []
+        for k, own, plane in each_part(*key):
+            turn = factors[1, *plane] * react[k]
             if twice:
                 turn = 2.0 * turn
-            nexts[slot].append(kept[4 * slot + k] + turn)
-            total_out[4 * slot + k] = total[4 * slot + k] + 2.0 * factors[4, plane] * react[k]
+            nexts[key].append(kept[own] + turn)
+            total_out[own] = total[own] + 2.0 * factors[4, *plane] * react[k]
     spectra_to(nexts, tabs.at[IX], send)
 
 
 def spectral_last(got, factors, total, tabs, send):
     spectra = spectra_of(got, tabs.at[FX])
-    nexts = [[], []]
-    for slot in range(2):
-        react = spectra[slot, 0]
-        for k, half, part in each_part():
-            plane = plane_of(slot, half, part)
-            nexts[slot].append(total[4 * slot + k] + factors[5, plane] * react[k])
+    nexts = {}
+    for key in PARTS:
+        (react,) = spectra[key]
+        nexts[key] = [
+            total[own] + factors[5, *plane] * react[k] for k, own, plane in each_part(*key)
+        ]
     spectra_to(nexts, tabs.at[IX], send)
 
 
-def phi_values(argument, degrees):
-    within = jnp.abs(argument) < 1.0
-    inside = jnp.where(within, argument, 0.0)
-    outside = jnp.where(within, 2.0, argument)
-    series = []
-    for degree in degrees:
-        running = jnp.zeros_like(argument) + 1.0 / math.factorial(11 + degree)
-        for exponent in range(10, -1, -1):
-            running = running * inside + 1.0 / math.factorial(exponent + degree)
-        series.append(running)
-    growth = jnp.exp(outside)
-    closed = [(growth - 1.0) / outside]
-    if len(degrees) > 1:
-        square = outside * outside
-        closed.append((growth - 1.0 - outside) / square)
-        closed.append((growth - 1.0 - outside - 0.5 * square) / (square * outside))
-    return [jnp.where(within, s, c) for s, c in zip(series, closed)]
+def step_factors(ksq):
+    lin = growth_rate - (1.0 - ksq) * (1.0 - ksq)
+    z = time_step * lin
+    e_half = jnp.exp(0.5 * z)
+    e_full = e_half * e_half
+    within = jnp.abs(z) < 1.0
+    inside = jnp.where(within, z, 0.0)
+    inverse = 1.0 / jnp.where(within, 2.0, z)
+    series = jnp.full_like(z, 1.0 / math.factorial(14))
+    for exponent in range(10, -1, -1):
+        series = series * inside + 1.0 / math.factorial(exponent + 3)
+    closed_one = (e_full - 1.0) * inverse
+    closed_two = (closed_one - 1.0) * inverse
+    third = jnp.where(within, series, (closed_two - 0.5) * inverse)
+    second = jnp.where(within, 0.5 + inside * series, closed_two)
+    first = jnp.where(within, 1.0 + inside * second, closed_one)
+    return (
+        e_half,
+        time_step * first / (e_half + 1.0),
+        e_full,
+        time_step * (first - 3.0 * second + 4.0 * third),
+        time_step * (second - 2.0 * third),
+        time_step * (4.0 * third - second),
+    )
 
 
 def factor_kernel(factors):
     device = lax.axis_index(BOTH)
     square = H * H
-    row = grid_of(0)
-    lane = grid_of(1)
     own = device * device
     alone = jnp.where(device == 0, 1, 0)
-    for plane in range(6):
-        half = plane % 2
-        slot = 1 if plane // 2 == 1 else 0
-        imaginary = plane // 2 == 2
+
+    def fill(plane, count):
+        row = lax.broadcasted_iota(jnp.int32, (count, H), 0)
+        lane = lax.broadcasted_iota(jnp.int32, (count, H), 1)
+        half, kind = plane % 2, plane // 2
+        lane0 = lane == 0
         modes = row * row
         if half:
             modes = jnp.where(row == 0, square, modes)
-        lane0 = lane == 0
-        if slot:
+        if kind == 1:
             modes = modes + own + alone * square
             modes = modes + jnp.where(lane0, (1 - alone) * square, lane * lane)
         else:
             modes = modes + own + lane * lane
-            pair = lane0 & (row == 0) if not half else (lane0 & (row != 0))
-            if imaginary and half:
-                pair = lane0
-            if half or imaginary:
+            pair = lane0 & (row != 0)
+            if kind == 2:
+                pair = lane0 if half else lane0 & (row == 0)
+            if half or kind == 2:
                 modes = modes + jnp.where(pair, alone * (2 * square), 0)
-        ksq = modes.astype(F32) * (wave_scale / N) ** 2
-        lin = growth_rate - (1.0 - ksq) * (1.0 - ksq)
-        scaled = time_step * lin
-        (half_phi,) = phi_values(0.5 * scaled, (1,))
-        first, second, third = phi_values(scaled, (1, 2, 3))
-        factors[0, plane] = jnp.exp(0.5 * scaled)
-        factors[1, plane] = 0.5 * time_step * half_phi
-        factors[2, plane] = jnp.exp(scaled)
-        factors[3, plane] = time_step * (first - 3.0 * second + 4.0 * third)
-        factors[4, plane] = time_step * (second - 2.0 * third)
-        factors[5, plane] = time_step * (4.0 * third - second)
+        values = step_factors(modes.astype(F32) * (wave_scale / N) ** 2)
+        for k in range(6):
+            factors[k, plane, pl.ds(0, count), :] = values[k]
+            if kind == 0:
+                factors[k, plane + 4, pl.ds(8, H - 8), :] = values[k][8:]
+
+    for plane in range(4):
+        fill(plane, H)
+    for plane in (4, 5):
+        fill(plane, 8)
 
 
 def shape(*dims):

time: 166 us -> 165 us (level)
  no operation moved by 1% of the time
where the time goes in v4:
time: 165 us
  blocking collectives  154 us (93%)
  Pallas kernels  11 us (7%)
    all_to_all x8, blocking collectives, move(): out = lax.all_to_all(tiles, BOTH, split_axis=0, concat_axis=0, tiled=True)  154 us
    pallas_call x9, Pallas kernels, call(): pl.pallas_call(kernel, out_shape=outs, in_specs=[ins] * len(args), out_sp...  11 us

profile of v4, /device:TPU:1, one launch (start us, length us, event | category | flops | bytes accessed | tf_op | source)
XLA Modules:
  0.0 165.1 jit_solution(125862621531076242)
XLA Ops:
  0.0 2.5 %first.1 = (f32[2048,128]{1,0:T(8,128)S(1)}, f32[6,6,128,128]{3,2,1,0:T(8,128)S(1)}, bf16[6,2,256,256]{3,2,1,0:T(8,128)(2,1)S(1)}) custom-call(f32[2,256,256]{2,1,0:T(8,128)} %field_hbm.1, bf16[6,2,256,256]{3,2,1,0:T(8,128)(2,1)} %constant.2.clone.tabs_hbm), custom_call_target="tpu_custom_call" | custom-call | tf_op jit(solution)/shard_map/first/pallas_call | solution.py:414
  2.5 30.2 %all_to_all.40 = f32[128,16,128]{2,1,0:T(8,128)S(1)} all-to-all(f32[128,16,128]{2,1,0:T(8,128)S(1)} %bitcast.28), channel_id=1, replica_groups=mesh['row'=8,'col'=16] {'row','col'}, dimensions={0} | all-to-all | bytes 2097152 | tf_op jit(solution)/shard_map/all_to_all | solution.py:427
  32.7 1.3 spectral_first.1
  34.1 17.7 %all_to_all.41 = f32[128,8,128]{2,1,0:T(8,128)S(1)} all-to-all(f32[128,8,128]{2,1,0:T(8,128)S(1)} %bitcast.29), channel_id=1, replica_groups=mesh['row'=8,'col'=16] {'row','col'}, dimensions={0} | all-to-all | bytes 1048576 | tf_op jit(solution)/shard_map/all_to_all | solution.py:427
  51.8 1.1 physical.3
  52.9 17.6 %all_to_all.42 = f32[128,8,128]{2,1,0:T(8,128)S(1)} all-to-all(f32[128,8,128]{2,1,0:T(8,128)S(1)} %bitcast.19), channel_id=1, replica_groups=mesh['row'=8,'col'=16] {'row','col'}, dimensions={0} | all-to-all | bytes 1048576 | tf_op jit(solution)/shard_map/all_to_all | solution.py:427
  70.6 0.8 spectral_middle.2
  71.4 17.6 %all_to_all.43 = f32[128,8,128]{2,1,0:T(8,128)S(1)} all-to-all(f32[128,8,128]{2,1,0:T(8,128)S(1)} %bitcast.30), channel_id=1, replica_groups=mesh['row'=8,'col'=16] {'row','col'}, dimensions={0} | all-to-all | bytes 1048576 | tf_op jit(solution)/shard_map/all_to_all | solution.py:427
  89.0 1.2 physical.4
  90.2 17.6 %all_to_all.44 = f32[128,8,128]{2,1,0:T(8,128)S(1)} all-to-all(f32[128,8,128]{2,1,0:T(8,128)S(1)} %bitcast.21), channel_id=1, replica_groups=mesh['row'=8,'col'=16] {'row','col'}, dimensions={0} | all-to-all | bytes 1048576 | tf_op jit(solution)/shard_map/all_to_all | solution.py:427
  107.8 0.8 spectral_middle.3
  108.7 17.6 %all_to_all.45 = f32[128,8,128]{2,1,0:T(8,128)S(1)} all-to-all(f32[128,8,128]{2,1,0:T(8,128)S(1)} %bitcast.31), channel_id=1, replica_groups=mesh['row'=8,'col'=16] {'row','col'}, dimensions={0} | all-to-all | bytes 1048576 | tf_op jit(solution)/shard_map/all_to_all | solution.py:427
  126.3 1.2 physical.5
  127.5 17.7 %all_to_all.46 = f32[128,8,128]{2,1,0:T(8,128)S(1)} all-to-all(f32[128,8,128]{2,1,0:T(8,128)S(1)} %bitcast.23), channel_id=1, replica_groups=mesh['row'=8,'col'=16] {'row','col'}, dimensions={0} | all-to-all | bytes 1048576 | tf_op jit(solution)/shard_map/all_to_all | solution.py:427
  145.1 0.7 spectral_last.1
  145.9 17.6 %all_to_all.47 = f32[128,8,128]{2,1,0:T(8,128)S(1)} all-to-all(f32[128,8,128]{2,1,0:T(8,128)S(1)} %bitcast.27), channel_id=1, replica_groups=mesh['row'=8,'col'=16] {'row','col'}, dimensions={0} | all-to-all | bytes 1048576 | tf_op jit(solution)/shard_map/all_to_all | solution.py:427
  163.5 1.4 last.1

commit v5 on v4

--- a/solution.py
+++ b/solution.py
@@ -65,15 +65,22 @@
     return jnp.dot(left, right, preferred_element_type=F32)
 
 
+def folded(whole):
+    count = whole.shape[0] // 2
+    return whole[:count], whole[count:]
+
+
 def table_left(table, parts, at=0, count=N):
     high, low = parts
     top, bottom = table[0, pl.ds(at, count), :], table[1, pl.ds(at, count), :]
-    return dot(top, high) + (dot(top, low) + dot(bottom, high))
+    main, rest = folded(dot(jnp.concatenate([top, bottom], axis=0), high))
+    return main + (rest + dot(top, low))
 
 
 def table_right(values, table):
     high, low = split(values)
-    return dot(high, table[0]) + (dot(low, table[0]) + dot(high, table[1]))
+    main, rest = folded(dot(jnp.concatenate([high, low], axis=0), table[0]))
+    return main + (rest + dot(high, table[1]))
 
 
 def grid_of(axis):

time: 165 us -> 165 us (level)
  no operation moved by 1% of the time
where the time goes in v5:
time: 165 us
  blocking collectives  154 us (93%)
  Pallas kernels  10.7 us (6%)
    all_to_all x8, blocking collectives, move(): out = lax.all_to_all(tiles, BOTH, split_axis=0, concat_axis=0, tiled=True)  154 us
    pallas_call x9, Pallas kernels, call(): pl.pallas_call(kernel, out_shape=outs, in_specs=[ins] * len(args), out_sp...  10.7 us

profile of v5, /device:TPU:1, one launch (start us, length us, event | category | flops | bytes accessed | tf_op | source)
XLA Modules:
  0.0 164.6 jit_solution(11844959996111328027)
XLA Ops:
  0.0 2.4 %first.1 = (f32[2048,128]{1,0:T(8,128)S(1)}, f32[6,6,128,128]{3,2,1,0:T(8,128)S(1)}, bf16[6,2,256,256]{3,2,1,0:T(8,128)(2,1)S(1)}) custom-call(f32[2,256,256]{2,1,0:T(8,128)} %field_hbm.1, bf16[6,2,256,256]{3,2,1,0:T(8,128)(2,1)} %constant.2.clone.tabs_hbm), custom_call_target="tpu_custom_call" | custom-call | tf_op jit(solution)/shard_map/first/pallas_call | solution.py:421
  2.4 30.2 %all_to_all.40 = f32[128,16,128]{2,1,0:T(8,128)S(1)} all-to-all(f32[128,16,128]{2,1,0:T(8,128)S(1)} %bitcast.28), channel_id=1, replica_groups=mesh['row'=8,'col'=16] {'row','col'}, dimensions={0} | all-to-all | bytes 2097152 | tf_op jit(solution)/shard_map/all_to_all | solution.py:434
  32.7 1.2 spectral_first.1
  33.9 17.7 %all_to_all.41 = f32[128,8,128]{2,1,0:T(8,128)S(1)} all-to-all(f32[128,8,128]{2,1,0:T(8,128)S(1)} %bitcast.29), channel_id=1, replica_groups=mesh['row'=8,'col'=16] {'row','col'}, dimensions={0} | all-to-all | bytes 1048576 | tf_op jit(solution)/shard_map/all_to_all | solution.py:434
  51.6 1.1 physical.3
  52.8 17.6 %all_to_all.42 = f32[128,8,128]{2,1,0:T(8,128)S(1)} all-to-all(f32[128,8,128]{2,1,0:T(8,128)S(1)} %bitcast.19), channel_id=1, replica_groups=mesh['row'=8,'col'=16] {'row','col'}, dimensions={0} | all-to-all | bytes 1048576 | tf_op jit(solution)/shard_map/all_to_all | solution.py:434
  70.4 0.8 spectral_middle.2
  71.2 17.6 %all_to_all.43 = f32[128,8,128]{2,1,0:T(8,128)S(1)} all-to-all(f32[128,8,128]{2,1,0:T(8,128)S(1)} %bitcast.30), channel_id=1, replica_groups=mesh['row'=8,'col'=16] {'row','col'}, dimensions={0} | all-to-all | bytes 1048576 | tf_op jit(solution)/shard_map/all_to_all | solution.py:434
  88.8 1.1 physical.4
  90.0 17.6 %all_to_all.44 = f32[128,8,128]{2,1,0:T(8,128)S(1)} all-to-all(f32[128,8,128]{2,1,0:T(8,128)S(1)} %bitcast.21), channel_id=1, replica_groups=mesh['row'=8,'col'=16] {'row','col'}, dimensions={0} | all-to-all | bytes 1048576 | tf_op jit(solution)/shard_map/all_to_all | solution.py:434
  107.6 0.8 spectral_middle.3
  108.4 17.7 %all_to_all.45 = f32[128,8,128]{2,1,0:T(8,128)S(1)} all-to-all(f32[128,8,128]{2,1,0:T(8,128)S(1)} %bitcast.31), channel_id=1, replica_groups=mesh['row'=8,'col'=16] {'row','col'}, dimensions={0} | all-to-all | bytes 1048576 | tf_op jit(solution)/shard_map/all_to_all | solution.py:434
  126.1 1.1 physical.5
  127.2 17.6 %all_to_all.46 = f32[128,8,128]{2,1,0:T(8,128)S(1)} all-to-all(f32[128,8,128]{2,1,0:T(8,128)S(1)} %bitcast.23), channel_id=1, replica_groups=mesh['row'=8,'col'=16] {'row','col'}, dimensions={0} | all-to-all | bytes 1048576 | tf_op jit(solution)/shard_map/all_to_all | solution.py:434
  144.8 0.7 spectral_last.1
  145.6 17.7 %all_to_all.47 = f32[128,8,128]{2,1,0:T(8,128)S(1)} all-to-all(f32[128,8,128]{2,1,0:T(8,128)S(1)} %bitcast.27), channel_id=1, replica_groups=mesh['row'=8,'col'=16] {'row','col'}, dimensions={0} | all-to-all | bytes 1048576 | tf_op jit(solution)/shard_map/all_to_all | solution.py:434
  163.2 1.4 last.1

commit v6 on v5

--- a/solution.py
+++ b/solution.py
@@ -190,13 +190,11 @@
 
     own = load(field_hbm, field, 0)
     loads = [load(tabs_hbm.at[k], tabs.at[k], 1 + k) for k in range(6)]
-    for one in (own, loads[FZ], loads[FY]):
+    for one in (own, *loads):
         one.start()
     factor_kernel(factors)
     for one in (own, loads[FZ], loads[FY]):
         one.wait()
-    for k in (FX, IX, IY, IZ):
-        loads[k].start()
     pieces = [field[row, pl.ds(H * half, H), :] for row, half in PIECES]
     to_messages([pieces, [reaction(v) for v in pieces]], send, tabs.at[FZ], tabs.at[FY])
     for k in (FX, IX, IY, IZ):
@@ -331,7 +329,7 @@
             if twice:
                 turn = 2.0 * turn
             nexts[key].append(kept[own] + turn)
-            total_out[own] = total[own] + 2.0 * factors[4, *plane] * react[k]
+            total_out[own] = total[own] + factors[4, *plane] * react[k]
     spectra_to(nexts, tabs.at[IX], send)
 
 
@@ -367,7 +365,7 @@
         time_step * first / (e_half + 1.0),
         e_full,
         time_step * (first - 3.0 * second + 4.0 * third),
-        time_step * (second - 2.0 * third),
+        2.0 * time_step * (second - 2.0 * third),
         time_step * (4.0 * third - second),
     )
 

time: 165 us -> 165 us (level)
  no operation moved by 1% of the time
where the time goes in v6:
time: 165 us
  blocking collectives  154 us (93%)
  Pallas kernels  10.7 us (6%)
    all_to_all x8, blocking collectives, move(): out = lax.all_to_all(tiles, BOTH, split_axis=0, concat_axis=0, tiled=True)  154 us
    pallas_call x9, Pallas kernels, call(): pl.pallas_call(kernel, out_shape=outs, in_specs=[ins] * len(args), out_sp...  10.7 us

profile of v6, /device:TPU:1, one launch (start us, length us, event | category | flops | bytes accessed | tf_op | source)
XLA Modules:
  0.0 164.6 jit_solution(11325061417919306928)
XLA Ops:
  0.0 2.4 %first.1 = (f32[2048,128]{1,0:T(8,128)S(1)}, f32[6,6,128,128]{3,2,1,0:T(8,128)S(1)}, bf16[6,2,256,256]{3,2,1,0:T(8,128)(2,1)S(1)}) custom-call(f32[2,256,256]{2,1,0:T(8,128)} %field_hbm.1, bf16[6,2,256,256]{3,2,1,0:T(8,128)(2,1)} %constant.2.clone.tabs_hbm), custom_call_target="tpu_custom_call" | custom-call | tf_op jit(solution)/shard_map/first/pallas_call | solution.py:419
  2.4 30.2 %all_to_all.40 = f32[128,16,128]{2,1,0:T(8,128)S(1)} all-to-all(f32[128,16,128]{2,1,0:T(8,128)S(1)} %bitcast.28), channel_id=1, replica_groups=mesh['row'=8,'col'=16] {'row','col'}, dimensions={0} | all-to-all | bytes 2097152 | tf_op jit(solution)/shard_map/all_to_all | solution.py:432
  32.7 1.2 spectral_first.1
  33.9 17.7 %all_to_all.41 = f32[128,8,128]{2,1,0:T(8,128)S(1)} all-to-all(f32[128,8,128]{2,1,0:T(8,128)S(1)} %bitcast.29), channel_id=1, replica_groups=mesh['row'=8,'col'=16] {'row','col'}, dimensions={0} | all-to-all | bytes 1048576 | tf_op jit(solution)/shard_map/all_to_all | solution.py:432
  51.6 1.1 physical.3
  52.8 17.6 %all_to_all.42 = f32[128,8,128]{2,1,0:T(8,128)S(1)} all-to-all(f32[128,8,128]{2,1,0:T(8,128)S(1)} %bitcast.19), channel_id=1, replica_groups=mesh['row'=8,'col'=16] {'row','col'}, dimensions={0} | all-to-all | bytes 1048576 | tf_op jit(solution)/shard_map/all_to_all | solution.py:432
  70.4 0.8 spectral_middle.2
  71.2 17.6 %all_to_all.43 = f32[128,8,128]{2,1,0:T(8,128)S(1)} all-to-all(f32[128,8,128]{2,1,0:T(8,128)S(1)} %bitcast.30), channel_id=1, replica_groups=mesh['row'=8,'col'=16] {'row','col'}, dimensions={0} | all-to-all | bytes 1048576 | tf_op jit(solution)/shard_map/all_to_all | solution.py:432
  88.9 1.1 physical.4
  90.0 17.6 %all_to_all.44 = f32[128,8,128]{2,1,0:T(8,128)S(1)} all-to-all(f32[128,8,128]{2,1,0:T(8,128)S(1)} %bitcast.21), channel_id=1, replica_groups=mesh['row'=8,'col'=16] {'row','col'}, dimensions={0} | all-to-all | bytes 1048576 | tf_op jit(solution)/shard_map/all_to_all | solution.py:432
  107.6 0.8 spectral_middle.3
  108.4 17.6 %all_to_all.45 = f32[128,8,128]{2,1,0:T(8,128)S(1)} all-to-all(f32[128,8,128]{2,1,0:T(8,128)S(1)} %bitcast.31), channel_id=1, replica_groups=mesh['row'=8,'col'=16] {'row','col'}, dimensions={0} | all-to-all | bytes 1048576 | tf_op jit(solution)/shard_map/all_to_all | solution.py:432
  126.1 1.1 physical.5
  127.2 17.6 %all_to_all.46 = f32[128,8,128]{2,1,0:T(8,128)S(1)} all-to-all(f32[128,8,128]{2,1,0:T(8,128)S(1)} %bitcast.23), channel_id=1, replica_groups=mesh['row'=8,'col'=16] {'row','col'}, dimensions={0} | all-to-all | bytes 1048576 | tf_op jit(solution)/shard_map/all_to_all | solution.py:432
  144.9 0.7 spectral_last.1
  145.6 17.7 %all_to_all.47 = f32[128,8,128]{2,1,0:T(8,128)S(1)} all-to-all(f32[128,8,128]{2,1,0:T(8,128)S(1)} %bitcast.27), channel_id=1, replica_groups=mesh['row'=8,'col'=16] {'row','col'}, dimensions={0} | all-to-all | bytes 1048576 | tf_op jit(solution)/shard_map/all_to_all | solution.py:432
  163.2 1.4 last.1

commit v7 on v6

--- a/solution.py
+++ b/solution.py
@@ -123,7 +123,7 @@
 
 
 def reaction(values):
-    return quadratic * values * values - values * values * values
+    return values * values * (quadratic - values)
 
 
 def send_modes(whole, piece, send, base):

time: 165 us -> 165 us (level)
  no operation moved by 1% of the time
where the time goes in v7:
time: 165 us
  blocking collectives  154 us (93%)
  Pallas kernels  10.7 us (6%)
    all_to_all x8, blocking collectives, move(): out = lax.all_to_all(tiles, BOTH, split_axis=0, concat_axis=0, tiled=True)  154 us
    pallas_call x9, Pallas kernels, call(): pl.pallas_call(kernel, out_shape=outs, in_specs=[ins] * len(args), out_sp...  10.7 us

profile of v7, /device:TPU:1, one launch (start us, length us, event | category | flops | bytes accessed | tf_op | source)
XLA Modules:
  0.0 164.6 jit_solution(14099268522407486420)
XLA Ops:
  0.0 2.4 %first.1 = (f32[2048,128]{1,0:T(8,128)S(1)}, f32[6,6,128,128]{3,2,1,0:T(8,128)S(1)}, bf16[6,2,256,256]{3,2,1,0:T(8,128)(2,1)S(1)}) custom-call(f32[2,256,256]{2,1,0:T(8,128)} %field_hbm.1, bf16[6,2,256,256]{3,2,1,0:T(8,128)(2,1)} %constant.2.clone.tabs_hbm), custom_call_target="tpu_custom_call" | custom-call | tf_op jit(solution)/shard_map/first/pallas_call | solution.py:419
  2.4 30.2 %all_to_all.40 = f32[128,16,128]{2,1,0:T(8,128)S(1)} all-to-all(f32[128,16,128]{2,1,0:T(8,128)S(1)} %bitcast.28), channel_id=1, replica_groups=mesh['row'=8,'col'=16] {'row','col'}, dimensions={0} | all-to-all | bytes 2097152 | tf_op jit(solution)/shard_map/all_to_all | solution.py:432
  32.7 1.2 spectral_first.1
  33.9 17.7 %all_to_all.41 = f32[128,8,128]{2,1,0:T(8,128)S(1)} all-to-all(f32[128,8,128]{2,1,0:T(8,128)S(1)} %bitcast.29), channel_id=1, replica_groups=mesh['row'=8,'col'=16] {'row','col'}, dimensions={0} | all-to-all | bytes 1048576 | tf_op jit(solution)/shard_map/all_to_all | solution.py:432
  51.6 1.1 physical.3
  52.8 17.6 %all_to_all.42 = f32[128,8,128]{2,1,0:T(8,128)S(1)} all-to-all(f32[128,8,128]{2,1,0:T(8,128)S(1)} %bitcast.19), channel_id=1, replica_groups=mesh['row'=8,'col'=16] {'row','col'}, dimensions={0} | all-to-all | bytes 1048576 | tf_op jit(solution)/shard_map/all_to_all | solution.py:432
  70.4 0.8 spectral_middle.2
  71.2 17.6 %all_to_all.43 = f32[128,8,128]{2,1,0:T(8,128)S(1)} all-to-all(f32[128,8,128]{2,1,0:T(8,128)S(1)} %bitcast.30), channel_id=1, replica_groups=mesh['row'=8,'col'=16] {'row','col'}, dimensions={0} | all-to-all | bytes 1048576 | tf_op jit(solution)/shard_map/all_to_all | solution.py:432
  88.8 1.1 physical.4
  90.0 17.6 %all_to_all.44 = f32[128,8,128]{2,1,0:T(8,128)S(1)} all-to-all(f32[128,8,128]{2,1,0:T(8,128)S(1)} %bitcast.21), channel_id=1, replica_groups=mesh['row'=8,'col'=16] {'row','col'}, dimensions={0} | all-to-all | bytes 1048576 | tf_op jit(solution)/shard_map/all_to_all | solution.py:432
  107.6 0.8 spectral_middle.3
  108.4 17.6 %all_to_all.45 = f32[128,8,128]{2,1,0:T(8,128)S(1)} all-to-all(f32[128,8,128]{2,1,0:T(8,128)S(1)} %bitcast.31), channel_id=1, replica_groups=mesh['row'=8,'col'=16] {'row','col'}, dimensions={0} | all-to-all | bytes 1048576 | tf_op jit(solution)/shard_map/all_to_all | solution.py:432
  126.1 1.1 physical.5
  127.2 17.6 %all_to_all.46 = f32[128,8,128]{2,1,0:T(8,128)S(1)} all-to-all(f32[128,8,128]{2,1,0:T(8,128)S(1)} %bitcast.23), channel_id=1, replica_groups=mesh['row'=8,'col'=16] {'row','col'}, dimensions={0} | all-to-all | bytes 1048576 | tf_op jit(solution)/shard_map/all_to_all | solution.py:432
  144.8 0.7 spectral_last.1
  145.6 17.6 %all_to_all.47 = f32[128,8,128]{2,1,0:T(8,128)S(1)} all-to-all(f32[128,8,128]{2,1,0:T(8,128)S(1)} %bitcast.27), channel_id=1, replica_groups=mesh['row'=8,'col'=16] {'row','col'}, dimensions={0} | all-to-all | bytes 1048576 | tf_op jit(solution)/shard_map/all_to_all | solution.py:432
  163.2 1.4 last.1
